TPU v7x, 32 devices: a whole 2x2x4 slice. The times are simulated.
32 devices in a mesh: dp: 8 (over z, y), tensor: 4 (over x, core).
Axes of the slice: x: 2, y: 2, z: 4, core: 2. Of those that a mesh axis runs over, the one named last changes fastest.
Arguments:
- layer_in: bfloat16 [16384, 768], P('dp'), may hold values from -6 to 6
- block_of: int32 [16, 1024], P('dp'), may hold values from 0 to 7, never falling along the last dimension, each value on 1 to 256 neighbouring positions
- block_links: int32 [16, 8, 8], P('dp'), may hold values 0 or 1
- w_query: bfloat16 [768, 768], P(None, 'tensor'), may hold values from -0.21875 to 0.21875
- b_query: float32 [768], P('tensor'), may hold values from -1.5 to 1.5
- w_key: bfloat16 [768, 768], P(None, 'tensor'), may hold values from -0.21875 to 0.21875
- w_value: bfloat16 [768, 768], P(None, 'tensor'), may hold values from -0.21875 to 0.21875
- b_value: float32 [768], P('tensor'), may hold values from -1.5 to 1.5
- w_out: bfloat16 [768, 768], P('tensor'), may hold values from -1.75 to 1.75
- b_out: float32 [768], replicated, may hold values from -1.5 to 1.5
- gain_one: float32 [768], replicated, may hold values from 0.5 to 1.5
- shift_one: float32 [768], replicated, may hold values from -1.5 to 1.5
- w_up: bfloat16 [768, 3072], P(None, 'tensor'), may hold values from -0.21875 to 0.21875
- b_up: float32 [3072], P('tensor'), may hold values from -1.5 to 1.5
- w_down: bfloat16 [3072, 768], P('tensor'), may hold values from -0.109375 to 0.109375
- b_down: float32 [768], replicated, may hold values from -1.5 to 1.5
- gain_two: float32 [768], replicated, may hold values from 0.5 to 1.5
- shift_two: float32 [768], replicated, may hold values from -1.5 to 1.5
- grad_out: bfloat16 [16384, 768], P(('dp', 'tensor')), may hold values from -6 to 6
Outputs:
- layer_out: bfloat16 [16384, 768], P(('dp', 'tensor'))
- grad_in: float32 [16384, 768], P(('dp', 'tensor'))
- grad_w_query: float32 [768, 768], P('dp', 'tensor')
- grad_b_query: float32 [768], P('tensor')
- grad_w_key: float32 [768, 768], P('dp', 'tensor')
- grad_w_value: float32 [768, 768], P('dp', 'tensor')
- grad_b_value: float32 [768], P('tensor')
- grad_w_out: float32 [768, 768], P('tensor', 'dp')
- grad_b_out: float32 [768], replicated
- grad_gain_one: float32 [768], replicated
- grad_shift_one: float32 [768], replicated
- grad_w_up: float32 [768, 3072], P('dp', 'tensor')
- grad_b_up: float32 [3072], P('tensor')
- grad_w_down: float32 [3072, 768], P('tensor', 'dp')
- grad_b_down: float32 [768], replicated
- grad_gain_two: float32 [768], replicated
- grad_shift_two: float32 [768], replicated
Inputs may be any that keep to these rules, and one draw needn't show every extreme that they name: `block_of`: within a sequence the block numbers never fall and all 8 blocks occur; each block has 1 to 256 positions and one has exactly 256. `block_links`: only entries [sequence, i, j] with j < i are read.
All inputs are finite; a program needn't handle non-finite values. No bound on the sum of `block_links` on one device may be relied on, other than what follows from the above.
Results may differ from a plain program's by a relative error of at most 0.018.
Values may be sent and summed in bfloat16 or wider, within the bound.
No kernel may reach another device: no remote copies, remote signals or barrier semaphores. Data moves between devices by JAX's collectives and lax.ppermute only.
A program may use at most 128 MiB of HBM per device.

v0:
```python
import functools

import jax
import jax.numpy as jnp
from jax import lax
from jax.experimental import pallas as pl
from jax.experimental.pallas import tpu as pltpu
from jax.sharding import PartitionSpec as P

D = 768
HEADS = 12
HEAD_DIM = D // HEADS

EPS = 1e-06
NEG = -1e30
ROOT_HALF = 0.7071067811865476
INV_ROOT_TWO_PI = 0.3989422804014327
BF16 = jnp.bfloat16
F32 = jnp.float32
BLOCK_MOST = 256
EXTRA = 8
COST_FLOPS = 50_000_000
COST_BYTES = 100_000
QTILE = 256
KTILE = 256
TILE = 256
SUMS = 8
ROWS = 128
HELD = True


def nn(left, right):
    return jnp.dot(left, right, preferred_element_type=F32)


def tn(left, right):
    return lax.dot_general(left, right, (((0,), (0,)), ((), ())), preferred_element_type=F32)


def nt(left, right):
    return lax.dot_general(left, right, (((1,), (1,)), ((), ())), preferred_element_type=F32)


VMEM = pl.BlockSpec(memory_space=pltpu.VMEM)
SMEM = pl.BlockSpec(memory_space=pltpu.SMEM)


def call(kernel, name, cost, scalars, arrays, outs, scratch=(), outside=()):
    arrays = [
        pltpu.with_memory_space_constraint(array, pltpu.HBM if index in outside else pltpu.VMEM)
        for index, array in enumerate(arrays)
    ]
    return pl.pallas_call(
        kernel,
        out_shape=tuple(
            pltpu.HBM(*out[:2]) if len(out) > 2 else pltpu.VMEM(*out) for out in outs
        ),
        in_specs=[SMEM] * len(scalars) + [VMEM] * len(arrays),
        out_specs=(VMEM,) * len(outs),
        scratch_shapes=list(scratch),
        cost_estimate=pl.CostEstimate(
            flops=int(cost * COST_FLOPS), bytes_accessed=int(cost * COST_BYTES), transcendentals=0
        ),
        name=name,
        compiler_params=pltpu.CompilerParams(
            vmem_limit_bytes=20 * 2**20
        ),
    )(*scalars, *arrays)


def pieces_of(column):
    high = column.astype(BF16).astype(F32)
    middle = (column - high).astype(BF16).astype(F32)
    return high, middle, column - high - middle


def with_pieces(base, lane, first, column):
    high, middle, low = pieces_of(column)
    base = jnp.where(lane == first, -high, base)
    base = jnp.where(lane == first + 1, -middle, base)
    return jnp.where(lane == first + 2, -low, base)


def lanes_of(head, rows):
    odd = lax.rem(head, 2)
    lane = lax.broadcasted_iota(jnp.int32, (rows, 2 * HEAD_DIM), 1)
    own = (lane >= HEAD_DIM * odd) & (lane < HEAD_DIM * (odd + 1))
    return odd, lane, own, HEAD_DIM * (1 - odd) + EXTRA


def forward_kernel(
    reach, place_ref, tokens_ref, w_query_ref, w_key_ref, w_value_ref, b_query_ref, b_value_ref,
    blocks_ref, links_ref, context_ref, query_ref, key_ref, value_ref,
    query_s, key_s, value_s, context_s, table_s, marks_s
):
    length = blocks_ref.shape[1]
    width = w_query_ref.shape[0]
    tiles = pl.cdiv(width, 128)
    chosen = place_ref[0]
    tokens = tokens_ref[pl.ds(pl.multiple_of(chosen * length, length), length)]
    for store, made in (
        (query_s, (nt(tokens, w_query_ref[...]) + b_query_ref[...]) * HEAD_DIM**-0.5),
        (key_s, nt(tokens, w_key_ref[...])),
        (value_s, nt(tokens, w_value_ref[...]) + b_value_ref[...]),
    ):
        for tile in range(tiles):
            last = min(128, width - 128 * tile)
            store[tile, :, :last] = made[:, 128 * tile : 128 * tile + last]

    row = blocks_ref[pl.ds(chosen, 1)].astype(F32)
    column = jnp.broadcast_to(row, (8, length)).T[:, :1]
    lane = lax.broadcasted_iota(jnp.int32, (length, 128), 1)
    onehot = jnp.where(column == lane.astype(F32), 1.0, 0.0)
    links = links_ref[chosen]
    count = links.shape[0]
    above = lax.broadcasted_iota(jnp.int32, (count, count), 0)
    below = lax.broadcasted_iota(jnp.int32, (count, count), 1)
    seen = (above == below) | ((above > below) & (links == 1))
    pairs = jnp.where(seen, 0.0, NEG).astype(BF16)
    sees = nn(onehot[:, :count].astype(BF16), pairs)
    table_s[...] = jnp.zeros_like(table_s)
    table_s[1, :, :count] = sees
    table_s[0, :, HEAD_DIM : HEAD_DIM + count] = sees
    ones = jnp.where((lane >= EXTRA) & (lane < EXTRA + 3), 1.0, onehot)
    marks_s[1] = ones
    marks_s[0] = pltpu.roll(ones, HEAD_DIM, 1)

    def one_head(head, carry):
        tile = head // 2
        odd, lane, own, first = lanes_of(head, length)
        marks = marks_s[odd]
        key_ref[head] = jnp.where(own, key_s[tile], marks).astype(BF16)
        ones = jnp.where((lane >= first) & (lane < first + 3), 1.0, 0.0)
        value_ref[head] = jnp.where(own, value_s[tile], ones).astype(BF16)
        odd, lane, own, first = lanes_of(head, QTILE)
        for start in range(0, length, QTILE):
            rows = slice(start, start + QTILE)
            seen = min(length, start + QTILE + reach)
            query = jnp.where(own, query_s[tile, rows], table_s[odd, rows])
            scores = nt(query.astype(BF16), key_ref[head, :seen])
            highest = jnp.max(scores, axis=-1, keepdims=True)
            weights = jnp.exp(scores - highest).astype(BF16)
            mixed = nn(weights, value_ref[head, :seen])
            total = jnp.sum(jnp.where(lane == first, mixed, 0.0), axis=-1, keepdims=True)
            context_s[tile, rows] = jnp.where(own, mixed * (1.0 / total), context_s[tile, rows])
            query_ref[head, rows] = with_pieces(
                query, lane, first, highest + jnp.log(total)
            ).astype(BF16)
        return carry

    lax.fori_loop(0, width // HEAD_DIM, one_head, 0)
    for tile in range(tiles):
        last = min(128, width - 128 * tile)
        context_ref[:, 128 * tile : 128 * tile + last] = context_s[tile, :, :last].astype(BF16)


def attend_forward(place, layer_in, weights, block_of, block_links):
    length = block_of.shape[1]
    width = weights[0].shape[0]
    heads = width // HEAD_DIM
    tiles = pl.cdiv(width, 128)
    big = ((heads, length, 128), BF16, HELD)
    tall = pltpu.VMEM((tiles, length, 128), F32)
    both = pltpu.VMEM((2, length, 128), F32)
    return call(
        functools.partial(forward_kernel, BLOCK_MOST),
        "attend_forward",
        8,
        [place],
        [layer_in, *weights, block_of, block_links],
        [((length, width), BF16), big, big, big],
        [tall] * 4 + [both] * 2,
        outside=range(1, 8),
    )


def backward_kernel(
    reach, core_ref, first_ref, second_ref, out_ref, w_query_ref, w_key_ref, w_value_ref,
    context_ref, query_ref, key_ref, value_ref, grads_ref, sums_ref, kept_ref, sent_ref, w_out_ref,
    grad_s, context_s, query_s, query_t, key_s, value_s, extended_s
):
    length, width = context_ref.shape
    half = length // 2
    tiles = pl.cdiv(width, 128)
    outward = jnp.zeros((width, out_ref.shape[1]), F32)
    for part, upstream_ref in enumerate((first_ref, second_ref)):
        begin = pl.multiple_of(lax.rem(core_ref[0] + part, 2) * half, half)
        rows = pl.ds(begin, half)
        upstream = upstream_ref[:half]
        made = nt(upstream, out_ref[...]).astype(BF16).astype(F32)
        context = context_ref[rows]
        outward += tn(context, upstream)
        aligned = made * context.astype(F32)
        for tile in range(tiles):
            last = min(128, width - 128 * tile)
            grad_s[tile, rows, :last] = made[:, 128 * tile : 128 * tile + last]
            context_s[tile, rows, :last] = aligned[:, 128 * tile : 128 * tile + last]
    w_out_ref[...] = outward

    def one_head(head, carry):
        tile = head // 2
        odd, lane, own, first = lanes_of(head, length)
        centre = jnp.sum(jnp.where(own, context_s[tile], 0.0), axis=-1, keepdims=True)
        grad = jnp.where(own, grad_s[tile], 0.0)
        extended_s[...] = with_pieces(grad, lane, first, centre).astype(BF16)
        odd, lane, own, first = lanes_of(head, KTILE)
        query_s[...] = jnp.zeros_like(query_s)
        for start in range(0, length, KTILE):
            rows = slice(start, start + KTILE)
            seen = max(0, start - reach)
            scores = nt(key_ref[head, rows], query_ref[head, seen:])
            probs = jnp.exp(scores)
            pulled = nt(value_ref[head, rows], extended_s[seen:])
            changed = (probs * pulled).astype(BF16)
            grad_value = nn(probs.astype(BF16), extended_s[seen:])
            grad_key = nn(changed, query_ref[head, seen:])
            value_s[tile, rows] = jnp.where(own, grad_value, value_s[tile, rows])
            key_s[tile, rows] = jnp.where(own, grad_key, key_s[tile, rows])
            query_s[seen:] += tn(changed, key_ref[head, rows])
        odd, lane, own, first = lanes_of(head, length)
        query_t[tile] = jnp.where(own, query_s[...] * HEAD_DIM**-0.5, query_t[tile])
        return carry

    lax.fori_loop(0, width // HEAD_DIM, one_head, 0)
    for kind, store in enumerate((query_t, key_s, value_s)):
        for tile in range(tiles):
            last = min(128, width - 128 * tile)
            made = store[tile, :, :last]
            begin = kind * width + 128 * tile
            grads_ref[:, begin : begin + last] = made.astype(BF16)
            if kind != 1:
                sums_ref[kind : kind + 1, 128 * tile : 128 * tile + last] = jnp.sum(
                    made, axis=0, keepdims=True
                )
    for begin, made_ref in ((1 - core_ref[0], sent_ref), (core_ref[0], kept_ref)):
        rows = pl.ds(pl.multiple_of(begin * half, half), half)
        inward = jnp.zeros(made_ref.shape, F32)
        for kind, weight_ref in enumerate((w_query_ref, w_key_ref, w_value_ref)):
            inward += nn(grads_ref[rows, kind * width : (kind + 1) * width], weight_ref[...])
        made_ref[...] = inward.astype(made_ref.dtype)


def attend_backward(core, upstream, out, weights, saved):
    length, width = saved[0].shape
    depth = out.shape[1]
    tall = pltpu.VMEM((pl.cdiv(width, 128), length, 128), F32)
    return call(
        functools.partial(backward_kernel, BLOCK_MOST),
        "attend_backward",
        12,
        [core],
        [*upstream, out, *weights, *saved],
        [
            ((length, 3 * width), BF16, HELD),
            ((3, width), F32),
            ((length // 2, depth), F32, HELD),
            ((length // 2, depth), BF16),
            ((width, depth), F32, HELD),
        ],
        [tall, tall, pltpu.VMEM((length, 128), F32), tall, tall, tall]
        + [pltpu.VMEM((length, 128), BF16)],
    )


def out_kernel(core_ref, mine_ref, other_ref, w_mine_ref, w_other_ref, far_ref, near_ref):
    width = mine_ref.shape[1]
    half = near_ref.shape[0]
    for begin, made_ref in ((1 - core_ref[0], far_ref), (core_ref[0], near_ref)):
        rows = pl.ds(pl.multiple_of(begin * half, half), half)
        made = nn(mine_ref[rows], w_mine_ref[...]) + nn(other_ref[rows], w_other_ref[:width])
        made_ref[...] = made.astype(made_ref.dtype)


def mean(values):
    return jnp.mean(values, axis=-1, keepdims=True)


def over_rows(count, rows, body, carry):
    def step(index, carry):
        return body(pl.multiple_of(index * rows, rows), carry)

    return lax.fori_loop(0, count // rows, step, carry)


def norm_one_kernel(
    place_ref, tokens_ref, near_ref, far_ref, bias_ref, gain_ref, shift_ref,
    hidden_ref, low_ref, held_ref, normed_ref, inverse_ref
):
    half = near_ref.shape[0]
    first = place_ref[0] * half

    def block(begin, carry):
        rows = pl.ds(begin, ROWS)
        tokens = tokens_ref[pl.ds(pl.multiple_of(first + begin, ROWS), ROWS)].astype(F32)
        values = tokens + near_ref[rows] + far_ref[rows].astype(F32) + bias_ref[...]
        centre = values - mean(values)
        inverse = lax.rsqrt(mean(centre * centre) + EPS)
        normed = centre * inverse
        hidden = normed * gain_ref[...] + shift_ref[...]
        hidden_ref[rows] = hidden
        low_ref[rows] = hidden.astype(BF16)
        held_ref[rows] = hidden.astype(BF16)
        normed_ref[rows] = normed
        inverse_ref[rows] = inverse
        return carry

    over_rows(half, ROWS, block, 0)


def gelu_into(up, rows, active_ref, held_ref, slope_ref):
    phi = 0.5 * (1.0 + lax.erf(up * ROOT_HALF))
    active = (up * phi).astype(BF16)
    active_ref[rows] = active
    held_ref[rows] = active
    slope_ref[rows] = phi + up * INV_ROOT_TWO_PI * jnp.exp(-0.5 * up * up)


def rise_kernel(
    mine_ref, other_ref, w_up_ref, bias_ref, active_ref, held_ref, slope_ref, other_held_ref
):
    half = mine_ref.shape[0]
    other_held_ref[...] = other_ref[...]
    for part, ref in enumerate((mine_ref, other_ref)):
        def tile(step, carry):
            begin = pl.multiple_of(step * TILE, TILE)
            up = nn(ref[pl.ds(begin, TILE)], w_up_ref[...]) + bias_ref[...]
            gelu_into(up, pl.ds(part * half + begin, TILE), active_ref, held_ref, slope_ref)
            return carry

        lax.fori_loop(0, half // TILE, tile, 0)


def join(order_ref, refs, joined_ref):
    rows = refs[0].shape[0]
    for step, ref in enumerate(refs):
        begin = jnp.bitwise_xor(order_ref[0], step) * rows
        joined_ref[pl.ds(pl.multiple_of(begin, rows), rows)] = ref[...]


def rise_other_kernel(
    order_ref, mine_ref, other_ref, *refs
):
    *pieces, out_ref, active_ref, held_ref, slope_ref, joined_ref = refs
    join(order_ref, pieces, joined_ref)
    bias = jnp.sum(out_ref[out_ref.shape[0] - 8 :].astype(F32), axis=0, keepdims=True)
    half = mine_ref.shape[0]
    for part, ref in enumerate((mine_ref, other_ref)):
        def tile(step, carry):
            begin = pl.multiple_of(step * TILE, TILE)
            up = nn(ref[pl.ds(begin, TILE)], joined_ref[...]) + bias
            gelu_into(up, pl.ds(part * half + begin, TILE), active_ref, held_ref, slope_ref)
            return carry

        lax.fori_loop(0, half // TILE, tile, 0)


def fall_kernel(order_ref, mine_ref, other_ref, w_down_ref, *refs):
    *pieces, near_ref, far_ref, joined_ref = refs
    half = near_ref.shape[0]
    join(order_ref, pieces, joined_ref)
    for begin, made_ref in ((half, far_ref), (0, near_ref)):
        def block(start, carry):
            part = pl.ds(begin + start, TILE)
            made = nn(mine_ref[part], w_down_ref[...]) + nn(other_ref[part], joined_ref[...])
            made_ref[pl.ds(start, TILE)] = made.astype(made_ref.dtype)
            return carry

        over_rows(half, TILE, block, 0)


def store_rows(sums_ref, rows):
    sums_ref[...] = jnp.zeros_like(sums_ref)
    for index, row in rows:
        sums_ref[index : index + 1] = row


def total(values):
    return jnp.sum(values, axis=0, keepdims=True)


def norm_two_kernel(
    hidden_ref, near_ref, far_ref, bias_ref, gain_ref, shift_ref, upstream_ref,
    layer_ref, grad_ref, low_ref, held_ref, sums_ref
):
    def block(begin, carry):
        rows = pl.ds(begin, ROWS)
        values = hidden_ref[rows] + near_ref[rows] + far_ref[rows].astype(F32) + bias_ref[...]
        centre = values - mean(values)
        inverse = lax.rsqrt(mean(centre * centre) + EPS)
        normed = centre * inverse
        layer_ref[rows] = (normed * gain_ref[...] + shift_ref[...]).astype(BF16)
        upstream = upstream_ref[rows].astype(F32)
        shaped = upstream * gain_ref[...]
        grad = inverse * (shaped - mean(shaped) - normed * mean(shaped * normed))
        grad_ref[rows] = grad
        low_ref[rows] = grad.astype(BF16)
        held_ref[rows] = grad.astype(BF16)
        made = (total(grad), total(upstream * normed), total(upstream))
        return tuple(old + new for old, new in zip(carry, made))

    zero = jnp.zeros((1, near_ref.shape[1]), F32)
    sums = over_rows(near_ref.shape[0], ROWS, block, (zero, zero, zero))
    store_rows(sums_ref, ((3, sums[0]), (4, sums[1]), (5, sums[2])))


def norm_one_back_kernel(
    grad_two_ref, near_ref, far_ref, normed_ref, inverse_ref, gain_ref, sums_two_ref, sums_up_ref,
    grad_ref, low_ref, sums_ref
):
    half = near_ref.shape[0]

    def block(begin, carry):
        rows = pl.ds(begin, ROWS)
        upstream = grad_two_ref[rows] + near_ref[rows] + far_ref[rows].astype(F32)
        normed = normed_ref[rows]
        shaped = upstream * gain_ref[...]
        grad = inverse_ref[rows] * (shaped - mean(shaped) - normed * mean(shaped * normed))
        grad_ref[rows] = grad
        low_ref[rows] = grad.astype(BF16)
        made = (total(grad), total(upstream * normed), total(upstream))
        return tuple(old + new for old, new in zip(carry, made))

    zero = jnp.zeros((1, near_ref.shape[1]), F32)
    sums = over_rows(half, ROWS, block, (zero, zero, zero))
    store_rows(
        sums_ref,
        (
            (0, sums[0]),
            (1, sums[1]),
            (2, sums[2]),
            (3, sums_two_ref[3:4]),
            (4, sums_two_ref[4:5]),
            (5, sums_two_ref[5:6]),
            (6, sums_up_ref[0:1]),
            (7, sums_up_ref[1:2]),
        ),
    )
    for term, rows in enumerate(pieces_of(sums_ref[...])):
        low_ref[half + term * SUMS : half + (term + 1) * SUMS] = rows.astype(BF16)


def ffn_back_kernel(
    mine_ref, other_ref, w_down_ref, joined_down_ref, slope_mine_ref, slope_other_ref,
    w_up_ref, joined_up_ref, low_mine_ref, low_other_ref, near_ref, far_ref, sums_ref, held_ref
):
    half = mine_ref.shape[0]
    held_ref[...] = other_ref[...]
    sums_ref[...] = jnp.zeros_like(sums_ref)
    for start, grads_ref, made_ref in ((half, other_ref, far_ref), (0, mine_ref, near_ref)):
        def tile(step, carry):
            begin = pl.multiple_of(step * TILE, TILE)
            rows = pl.ds(start + begin, TILE)
            grads = grads_ref[pl.ds(begin, TILE)]
            made = jnp.zeros((TILE, near_ref.shape[1]), F32)
            for index, (down_ref, slope_ref, up_ref, low_ref) in enumerate(
                (
                    (w_down_ref, slope_mine_ref, w_up_ref, low_mine_ref),
                    (joined_down_ref, slope_other_ref, joined_up_ref, low_other_ref),
                )
            ):
                grad = nt(grads, down_ref[...]) * slope_ref[rows]
                sums_ref[index : index + 1] += total(grad)
                low = grad.astype(BF16)
                low_ref[rows] = low
                made += nt(low, up_ref[...])
            made_ref[pl.ds(begin, TILE)] = made.astype(made_ref.dtype)
            return carry

        lax.fori_loop(0, half // TILE, tile, 0)


def weight_grads_kernel(
    bit, place_ref, left_mine_ref, left_other_ref, mine_ref, other_ref,
    kept_mine_ref, kept_other_ref, sent_mine_ref, sent_other_ref, whole_s
):
    half = left_mine_ref.shape[0]
    count, share = kept_mine_ref.shape[:2]
    own = place_ref[0]
    for right_ref, kept_ref, sent_ref in (
        (mine_ref, kept_mine_ref, sent_mine_ref), (other_ref, kept_other_ref, sent_other_ref)
    ):
        def block(begin, carry, right_ref=right_ref):
            columns = pl.ds(begin, TILE)
            whole_s[columns] = tn(left_mine_ref[:, columns], right_ref[:half]) + tn(
                left_other_ref[:, columns], right_ref[half:]
            )
            return carry

        over_rows(whole_s.shape[0], TILE, block, 0)
        for member in range(count):
            base = member % bit + member // bit * 2 * bit
            for parity, made_ref in ((own, kept_ref), (1 - own, sent_ref)):
                begin = pl.multiple_of((base + bit * parity) * share, 8)
                made_ref[member] = whole_s[pl.ds(begin, share)].astype(made_ref.dtype)


def combine_kernel(up_ref, up_received_ref, down_ref, down_received_ref, made_ref):
    count = up_ref.shape[0]
    for kind, (kept_ref, received_ref) in enumerate(
        ((up_ref, up_received_ref), (down_ref, down_received_ref))
    ):
        for member in range(count):
            made = kept_ref[member] + received_ref[member].astype(F32)
            made_ref[kind * count + member] = made.astype(BF16)


def split_kernel(
    members_ref, up_ref, up_received_ref, down_ref, down_received_ref, across_ref, *refs
):
    count = up_ref.shape[0]
    for kind, (kept_ref, received_ref) in enumerate(
        ((up_ref, up_received_ref), (down_ref, down_received_ref))
    ):
        for step in range(count):
            index = jnp.bitwise_xor(members_ref[kind], step)
            made = kept_ref[index] + received_ref[index].astype(F32)
            made += across_ref[kind * count + index].astype(F32)
            refs[kind * count + step][...] = made.astype(BF16)


def three_sums(values, first):
    return (
        values[first : first + SUMS]
        + values[first + SUMS : first + 2 * SUMS]
        + values[first + 2 * SUMS : first + 3 * SUMS]
    )


def qkv_split_kernel(members_ref, kept_ref, received_ref, *refs):
    count, rows = kept_ref.shape[:2]
    share = rows - 3 * SUMS
    for step in range(count):
        index = jnp.bitwise_xor(members_ref[0], step)
        made_ref = refs[step]
        made = kept_ref[index] + received_ref[index].astype(F32)
        made_ref[:share] = made[:share].astype(BF16)
        for term, part in enumerate(pieces_of(three_sums(made, share))):
            made_ref[share + term * SUMS : share + (term + 1) * SUMS] = part.astype(BF16)


def added(refs):
    made = refs[0][...].astype(F32)
    for ref in refs[1:]:
        made += ref[...].astype(F32)
    return made


def finish_kernel(*refs):
    *terms, query_ref, key_ref, value_ref, out_ref, bias_ref, sums_ref, up_ref, down_ref = refs
    count = len(terms) // 3
    share, width = query_ref.shape
    up_ref[...] = added(terms[:count])
    down_ref[...] = added(terms[count : 2 * count])
    made = added(terms[2 * count :])
    query_ref[...] = made[:share, :width]
    key_ref[...] = made[:share, width : 2 * width]
    value_ref[...] = made[:share, 2 * width : 3 * width]
    out_ref[...] = made[:share, 3 * width :].T
    sums = three_sums(made, share)
    sums_ref[...] = sums
    bias_ref[...] = sums[7:8]


def sum_kernel(*refs):
    *terms, made_ref = refs
    made = terms[0][...].astype(F32)
    for term in terms[1:]:
        made += term[...].astype(F32)
    made_ref[...] = made.astype(made_ref.dtype)


def qkv_pieces_kernel(
    place_ref, parity_ref, tokens_ref, near_ref, far_ref, sums_near_ref, sums_far_ref,
    out_near_ref, out_far_ref, norm_sums_ref, mine_ref, partner_ref, across_ref, diagonal_ref,
    kept_ref, sent_ref, whole_s
):
    count, rows = kept_ref.shape[:2]
    share = rows - 3 * SUMS
    length, columns = near_ref.shape
    width = out_near_ref.shape[0]
    half = mine_ref.shape[0] - 3 * SUMS
    made = jnp.zeros((tokens_ref.shape[1], columns), F32)
    for chosen, low_ref in ((place_ref[0], near_ref), (1 - place_ref[0], far_ref)):
        tokens = tokens_ref[pl.ds(pl.multiple_of(chosen * length, length), length)]
        made += tn(tokens, low_ref[...])
    whole_s[:, :columns] = made
    whole_s[:, columns:] = (out_near_ref[...] + out_far_ref[...]).T

    def sums_of(ref):
        terms = [ref[half + k * SUMS : half + (k + 1) * SUMS].astype(F32) for k in range(3)]
        return terms[0] + terms[1] + terms[2]

    across = sums_of(across_ref)
    sums = norm_sums_ref[...]
    row = lax.broadcasted_iota(jnp.int32, sums.shape, 0)
    bias = sums_near_ref[...] + sums_far_ref[...]
    lane = lax.broadcasted_iota(jnp.int32, (1, columns + width), 1)
    biases = jnp.concatenate(
        [bias[0:1], bias[1:2], bias[2:3], jnp.zeros((1, width), F32)], axis=1
    )
    biases = jnp.where((lane < width) | (lane >= 2 * width), biases, 0.0)
    sums = jnp.where(
        row < 6,
        sums + sums_of(partner_ref) + across + sums_of(diagonal_ref),
        jnp.where(row == 6, sums + across[7:8], biases),
    )
    terms = pieces_of(sums)
    for member in range(count):
        for parity, made_ref in ((parity_ref[0], kept_ref), (1 - parity_ref[0], sent_ref)):
            begin = pl.multiple_of((2 * member + parity) * share, 8)
            made_ref[member, :share] = whole_s[pl.ds(begin, share)].astype(made_ref.dtype)
            for k, term in enumerate(terms):
                made_ref[member, share + k * SUMS : share + (k + 1) * SUMS] = term.astype(
                    made_ref.dtype
                )


def swap_tensor(array, mask):
    ways = lax.axis_size("tensor")
    return lax.ppermute(array, "tensor", [(i, i ^ mask) for i in range(ways)])


def swap_dp(array, mask):
    ways = lax.axis_size("dp")
    return lax.ppermute(array, "dp", [(i, i ^ mask) for i in range(ways)])


def across(array):
    return swap_tensor(array, 2)


def partner(array):
    return swap_tensor(array, 1)


def after(array, *earlier):
    return lax.optimization_barrier((array,) + earlier)[0]


def three_terms(row):
    high = lax.reduce_precision(row, 8, 7)
    middle = lax.reduce_precision(row - high, 8, 7)
    terms = jnp.stack([high, middle, row - high - middle]).astype(BF16)
    return jnp.pad(terms, ((0, 5), (0, 0)))


def on_device(
    layer_in,
    block_of,
    block_links,
    w_query,
    b_query,
    w_key,
    w_value,
    b_value,
    w_out,
    b_out,
    gain_one,
    shift_one,
    w_up,
    b_up,
    w_down,
    b_down,
    gain_two,
    shift_two,
    grad_out,
):
    length = block_of.shape[1]
    half = length // 2
    place = lax.axis_index("tensor")
    sequence = place // 2
    core = place % 2
    width = w_query.shape[1]
    hidden = w_up.shape[1]
    ways = lax.axis_size("dp")
    share = D // ways
    group = lax.axis_index("dp")

    def scalar(value):
        return jnp.full((1,), value, jnp.int32)

    def row(vector):
        return vector.reshape(1, -1)

    def part_of(array, parts):
        rows = array.shape[0] // parts
        return lax.dynamic_slice_in_dim(array, group % parts * rows, rows, 0)

    def spread(part, parts):
        return [swap_dp(part, step) for step in range(1, parts)]

    out_received = across(jnp.concatenate([w_out, three_terms(b_up)], axis=0))
    up_part = across(part_of(w_up, 4))
    down_part = across(part_of(w_down, 4))

    weights = (w_query.T, w_key.T, w_value.T)
    inputs = weights + (row(b_query), row(b_value))
    near_place, far_place = scalar(sequence), scalar(1 - sequence)
    up_parts = spread(up_part, 4)
    saved_far = attend_forward(
        after(far_place, up_part), layer_in, inputs, block_of, block_links
    )
    context_other = across(saved_far[0])
    down_parts = spread(down_part, 4)
    saved_near = attend_forward(
        after(near_place, saved_far[0], down_part, *up_parts), layer_in, inputs, block_of, block_links
    )

    here = scalar(core)
    far, near = call(
        out_kernel,
        "out",
        2,
        [here],
        [after(saved_near[0], *down_parts), context_other, w_out, out_received],
        [((half, D), BF16), ((half, D), F32)],
    )
    hidden_one, hidden_mine, hidden_held, normed_one, inverse_one = call(
        norm_one_kernel,
        "norm_one",
        1,
        [scalar(place)],
        [layer_in, near, partner(far), row(b_out), row(gain_one), row(shift_one)],
        [((half, D), F32), ((half, D), BF16), ((half, D), BF16, HELD)]
        + [((half, D), F32), ((half, 1), F32)],
    )
    hidden_partner = partner(hidden_mine)
    active_mine, active_held, slope_mine, hidden_partner_held = call(
        rise_kernel,
        "rise_mine",
        2.6,
        [],
        [hidden_mine, hidden_partner, w_up, row(b_up)],
        [((length, hidden), BF16), ((length, hidden), BF16, HELD), ((length, hidden), F32)]
        + [((half, D), BF16, HELD)],
    )
    active_other, active_other_held, slope_other, up_other = call(
        rise_other_kernel,
        "rise_other",
        4,
        [scalar(group % 4)],
        [after(hidden_mine, active_mine), hidden_partner, up_part, *up_parts, out_received],
        [((length, hidden), BF16), ((length, hidden), BF16, HELD), ((length, hidden), F32)]
        + [(w_up.shape, BF16)],
    )
    near, far, down_whole = call(
        fall_kernel,
        "fall",
        2.7,
        [scalar(group % 4)],
        [active_mine, active_other, w_down, down_part, *down_parts],
        [((half, D), F32), ((half, D), BF16), (w_down.shape, BF16)],
    )
    layer_out, grad_two, ffn_mine, ffn_held, sums_two = call(
        norm_two_kernel,
        "norm_two",
        1.5,
        [],
        [hidden_one, near, partner(far), row(b_down), row(gain_two), row(shift_two), grad_out],
        [((half, D), BF16, HELD), ((half, D), F32), ((half, D), BF16), ((half, D), BF16, HELD)]
        + [((SUMS, D), F32)],
    )
    ffn_partner = partner(ffn_mine)
    low_mine, low_other, near, far, sums_up, ffn_partner_held = call(
        ffn_back_kernel,
        "ffn_back",
        7,
        [],
        [ffn_mine, ffn_partner, w_down, down_whole, slope_mine, slope_other, w_up, up_other],
        [((length, hidden), BF16, HELD)] * 2
        + [((half, D), F32), ((half, D), BF16), ((SUMS, hidden), F32), ((half, D), BF16, HELD)],
    )
    count = ways // 2

    def weight_grads(name, bit, left, right, outside):
        return call(
            functools.partial(weight_grads_kernel, bit),
            name,
            4,
            [scalar(group // bit % 2)],
            [*left, *right],
            [((count, share, hidden), F32, HELD)] * 2 + [((count, share, hidden), BF16, HELD)] * 2,
            [pltpu.VMEM((D, hidden), F32)],
            outside=outside,
        )

    up_mine, up_other, up_mine_sent, up_other_sent = weight_grads(
        "up_grads", 1, (hidden_held, hidden_partner_held), (low_mine, low_other), range(4)
    )
    up_other_received = swap_dp(up_other_sent, 1)
    down_mine, down_other, down_mine_sent, down_other_sent = weight_grads(
        "down_grads",
        2,
        (after(ffn_held, up_other_sent), ffn_partner_held),
        (active_held, active_other_held),
        range(4),
    )
    down_other_received = swap_dp(down_other_sent, 2)
    grad_one, one_mine, sums = call(
        norm_one_back_kernel,
        "norm_one_back",
        1.1,
        [],
        [grad_two, after(near, down_other_sent), partner(far), normed_one, inverse_one]
        + [row(gain_one), sums_two, sums_up],
        [((half, D), F32, HELD), ((half + 3 * SUMS, D), BF16, HELD), ((SUMS, D), F32)],
    )
    one_partner = partner(one_mine)
    one_across = across(one_mine)

    low_near, columns_near, near_kept, near_sent, out_near = attend_backward(
        here, (one_mine, one_partner), w_out, weights, saved_near
    )
    (other,) = call(
        combine_kernel,
        "combine",
        100,
        [],
        [up_other, after(up_other_received, low_near), down_other, down_other_received],
        [((ways, share, hidden), BF16, HELD)],
        outside=range(4),
    )
    across_partner = partner(after(one_across, low_near))
    other_received = across(other)
    near_received = partner(after(near_sent, other))
    up_mine_received = swap_dp(after(up_mine_sent, low_near), 1)
    down_mine_received = swap_dp(after(down_mine_sent, low_near), 2)
    low_far, columns_far, far_kept, far_sent, out_far = attend_backward(
        here, (one_across, after(across_partner, other)), w_out, weights, saved_far
    )
    qkv_kept, qkv_sent = call(
        qkv_pieces_kernel,
        "qkv_pieces",
        3.7,
        [after(near_place, up_mine_received, down_mine_received, other_received), scalar(group % 2)],
        [layer_in, low_near, low_far, columns_near, columns_far, out_near, out_far, sums]
        + [one_mine, one_partner, one_across, across_partner],
        [((count, share + 3 * SUMS, 4 * width), F32, HELD)]
        + [((count, share + 3 * SUMS, 4 * width), BF16, HELD)],
        [pltpu.VMEM((D, 4 * width), F32)],
        outside=range(1, 8),
    )
    qkv_received = swap_dp(qkv_sent, 1)
    (in_far,) = call(
        sum_kernel,
        "sum_far",
        0.7,
        [],
        [far_kept, partner(after(far_sent, qkv_kept))],
        [((half, D), BF16, HELD)],
        outside=range(2),
    )
    in_other = across(in_far)
    members = jnp.stack([group // 2, group // 4 * 2 + group % 2]).astype(jnp.int32)
    terms = call(
        split_kernel,
        "split",
        1,
        [members],
        [up_mine, up_mine_received, down_mine, down_mine_received]
        + [other_received],
        [((share, hidden), BF16, HELD)] * ways,
        outside=range(5),
    )
    qkv_terms = call(
        qkv_split_kernel,
        "qkv_split",
        1,
        [members],
        [qkv_kept, qkv_received],
        [((share + 3 * SUMS, 4 * width), BF16, HELD)] * count,
        outside=range(2),
    )
    swapped = [
        terms[step] if step == 0 else swap_dp(terms[step], 2 * step) for step in range(count)
    ] + [
        terms[count + step]
        if step == 0
        else swap_dp(terms[count + step], step // 2 * 4 + step % 2)
        for step in range(count)
    ]
    swapped += [
        qkv_terms[step] if step == 0 else swap_dp(qkv_terms[step], 2 * step)
        for step in range(count)
    ]
    (grad_in,) = call(
        sum_kernel,
        "sum_in",
        1,
        [],
        [grad_one, near_kept, near_received, in_other],
        [((half, D), F32, HELD)],
        outside=range(4),
    )
    grad_query, grad_key, grad_value, grad_w_out, bias_sums, sums, grad_w_up, grad_w_down = call(
        finish_kernel,
        "finish",
        1.5,
        [],
        [after(swapped[0], grad_in), *swapped[1:]],
        [((share, width), F32, HELD)] * 3
        + [((width, share), F32, HELD), ((1, 4 * width), F32), ((SUMS, D), F32)]
        + [((share, hidden), F32, HELD), ((share, hidden), F32, HELD)],
        outside=range(ways + count),
    )
    bias_sums = bias_sums.reshape(-1)
    return (
        layer_out,
        grad_in,
        grad_query,
        bias_sums[:width],
        grad_key,
        grad_value,
        bias_sums[2 * width : 3 * width],
        grad_w_out,
        sums[0],
        sums[1],
        sums[2],
        grad_w_up,
        sums[6],
        grad_w_down.T,
        sums[3],
        sums[4],
        sums[5],
    )


def solution(mesh):
    in_specs = (
        P("dp", None),
        P("dp", None),
        P("dp", None, None),
        P(None, "tensor"),
        P("tensor"),
        P(None, "tensor"),
        P(None, "tensor"),
        P("tensor"),
        P("tensor", None),
        P(),
        P(),
        P(),
        P(None, "tensor"),
        P("tensor"),
        P("tensor", None),
        P(),
        P(),
        P(),
        P(("dp", "tensor"), None),
    )
    out_specs = (
        P(("dp", "tensor"), None),
        P(("dp", "tensor"), None),
        P("dp", "tensor"),
        P("tensor"),
        P("dp", "tensor"),
        P("dp", "tensor"),
        P("tensor"),
        P("tensor", "dp"),
        P(),
        P(),
        P(),
        P("dp", "tensor"),
        P("tensor"),
        P("tensor", "dp"),
        P(),
        P(),
        P(),
    )
    return jax.shard_map(
        on_device, mesh=mesh, in_specs=in_specs, out_specs=out_specs, check_vma=False
    )
```

profile of v0, /device:TPU:0, one launch (start us, length us, event | category | flops | bytes accessed | tf_op | source)
XLA Modules:
  0.0 226.8 jit_solution(18387972127226143706)
XLA Ops:
  1.7 3.0 %collective-permute-start = (bf16[192,768]{1,0:T(8,128)(2,1)S(1)}, bf16[192,768]{1,0:T(8,128)(2,1)}, u32[]{:S(2)}, u32[]{:S(2)}) collective-permute-start(bf16[192,768]{1,0:T(8,128)(2,1)S(1)} %constant_dynamic-slice_fusion.1), channel_id=1, source_target_pairs={{0,2},{1,3},{2,0},{3,1},{4,6},{5,7},{6,4},{7,5},{8,10},{9,11},{10,... | collective-permute-start | bytes 884744 | tf_op jit(solution)/shard_map/ppermute | solution.py:620
  6.4 6.2 %collective-permute-done.refs_0_ = bf16[192,768]{1,0:T(8,128)(2,1)} collective-permute-done((bf16[192,768]{1,0:T(8,128)(2,1)S(1)}, bf16[192,768]{1,0:T(8,128)(2,1)}, u32[]{:S(2)}, u32[]{:S(2)}) %collective-permute-start) | collective-permute-done | bytes 294944 | tf_op jit(solution)/shard_map/ppermute | solution.py:620
  12.7 3.1 %collective-permute-start.4 = (bf16[192,768]{1,0:T(8,128)(2,1)}, bf16[192,768]{1,0:T(8,128)(2,1)}, u32[]{:S(2)}, u32[]{:S(2)}) collective-permute-start(bf16[192,768]{1,0:T(8,128)(2,1)} %collective-permute-done.refs_0_), channel_id=1, source_target_pairs={{0,12},{4,8},{8,4},{12,0},{16,28},{20,24},{24,20},{28,16},{1,13},{... | collective-permute-start | bytes 884744 | tf_op jit(solution)/shard_map/ppermute | solution.py:625
  18.9 10.7 %attend_forward.2 = (bf16[1024,192]{1,0:T(8,128)(2,1)}, bf16[3,1024,128]{2,1,0:T(8,128)(2,1)}, bf16[3,1024,128]{2,1,0:T(8,128)(2,1)}, bf16[3,1024,128]{2,1,0:T(8,128)(2,1)}) custom-call(s32[1]{0:T(128)} %bitcast.3.place_ref, bf16[2048,768]{1,0:T(8,128)(2,1)S(1)} %copy-done, bf16[192,768]{1,0:T(8,128)(2,1)} %bitcast.17, bf16[192,768]{1,0:T(8,128)(2,1)} %bitcast.21, ...), custom_call_target="tpu_custom_call" | custom-call | flops 400000000 | bytes 800000 | tf_op jit(solution)/shard_map/attend_forward/pallas_call | solution.py:53
  32.4 2.9 %collective-permute-start.7 = (bf16[192,768]{1,0:T(8,128)(2,1)}, bf16[192,768]{1,0:T(8,128)(2,1)}, u32[]{:S(2)}, u32[]{:S(2)}) collective-permute-start(bf16[192,768]{1,0:T(8,128)(2,1)} %collective-permute-done.1.refs_0_), channel_id=1, source_target_pairs={{0,12},{4,8},{8,4},{12,0},{16,28},{20,24},{24,20},{28,16},{1,13},{... | collective-permute-start | bytes 884744 | tf_op jit(solution)/shard_map/ppermute | solution.py:625
  36.0 10.3 %attend_forward.3 = (bf16[1024,192]{1,0:T(8,128)(2,1)S(1)}, bf16[3,1024,128]{2,1,0:T(8,128)(2,1)}, bf16[3,1024,128]{2,1,0:T(8,128)(2,1)}, bf16[3,1024,128]{2,1,0:T(8,128)(2,1)}) custom-call(s32[1]{0:T(128)} %bitcast.2.place_ref, bf16[2048,768]{1,0:T(8,128)(2,1)S(1)} %copy-done.1, bf16[192,768]{1,0:T(8,128)(2,1)} %bitcast.18, bf16[192,768]{1,0:T(8,128)(2,1)} %bitcast.22, ...), custom_call_target="tpu_custom_call" | custom-call | flops 400000000 | bytes 800000 | tf_op jit(solution)/shard_map/attend_forward/pallas_call | solution.py:53
  50.0 2.2 collective-permute-done.10.far_ref
  54.4 2.1 collective-permute-done.11.other_ref
  56.5 3.8 %rise_mine.1 = (bf16[1024,768]{1,0:T(8,128)(2,1)S(1)}, bf16[1024,768]{1,0:T(8,128)(2,1)}, f32[1024,768]{1,0:T(8,128)S(1)}, bf16[512,768]{1,0:T(8,128)(2,1)}) custom-call(bf16[512,768]{1,0:T(8,128)(2,1)S(1)} %get-tuple-element.122.mine_ref, bf16[512,768]{1,0:T(8,128)(2,1)S(1)} %collective-permute-done.11.other_ref, bf16[768,768]{1,0:T(8,128)(2,1)S(1)} %copy-done.2, ...), custom_call_target="tpu_custom_call" | custom-call | flops 130000000 | bytes 260000 | tf_op jit(solution)/shard_map/rise_mine/pallas_call | solution.py:53
  60.3 5.3 %rise_other.1 = (bf16[1024,768]{1,0:T(8,128)(2,1)S(1)}, bf16[1024,768]{1,0:T(8,128)(2,1)}, f32[1024,768]{1,0:T(8,128)S(1)}, bf16[768,768]{1,0:T(8,128)(2,1)S(1)}) custom-call(s32[1]{0:T(128)} %bitcast.9.order_ref, bf16[512,768]{1,0:T(8,128)(2,1)S(1)} %get-tuple-element.122.mine_ref, bf16[512,768]{1,0:T(8,128)(2,1)S(1)} %collective-permute-done.11.other_ref, ...), custom_call_target="tpu_custom_call" | custom-call | flops 200000000 | bytes 400000 | tf_op jit(solution)/shard_map/rise_other/pallas_call | solution.py:53
  65.6 4.5 %fall.1 = (f32[512,768]{1,0:T(8,128)S(1)}, bf16[512,768]{1,0:T(8,128)(2,1)S(1)}, bf16[768,768]{1,0:T(8,128)(2,1)S(1)}) custom-call(s32[1]{0:T(128)} %bitcast.9.order_ref, bf16[1024,768]{1,0:T(8,128)(2,1)S(1)} %get-tuple-element.121.mine_ref, bf16[1024,768]{1,0:T(8,128)(2,1)S(1)} %get-tuple-element.123.other_ref, bf16[768,768]{1,0:T(8,128)(2,1)S(1)} %copy-done.3, ...), custom_call_target="tpu_custom_call" | custom-call | flops 135000000 | bytes 270000 | tf_op jit(solution)/shard_map/fall/pallas_call | solution.py:53
  72.5 2.7 %norm_two.1 = (bf16[512,768]{1,0:T(8,128)(2,1)}, f32[512,768]{1,0:T(8,128)S(1)}, bf16[512,768]{1,0:T(8,128)(2,1)S(1)}, bf16[512,768]{1,0:T(8,128)(2,1)}, f32[8,768]{1,0:T(8,128)S(1)}) custom-call(f32[512,768]{1,0:T(8,128)S(1)} %get-tuple-element.119.hidden_ref, f32[512,768]{1,0:T(8,128)S(1)} %get-tuple-element.124.near_ref, ...), custom_call_target="tpu_custom_call" | custom-call | flops 75000000 | bytes 150000 | tf_op jit(solution)/shard_map/norm_two/pallas_call | solution.py:53
  75.3 2.1 collective-permute-done.13.other_ref
  77.5 8.3 %ffn_back.1 = (bf16[1024,768]{1,0:T(8,128)(2,1)}, bf16[1024,768]{1,0:T(8,128)(2,1)}, f32[512,768]{1,0:T(8,128)S(1)}, bf16[512,768]{1,0:T(8,128)(2,1)}, f32[8,768]{1,0:T(8,128)S(1)}, /*index=5*/bf16[512,768]{1,0:T(8,128)(2,1)}) custom-call(bf16[512,768]{1,0:T(8,128)(2,1)S(1)} %get-tuple-element.128.mine_ref, ...), custom_call_target="tpu_custom_call" | custom-call | flops 350000000 | bytes 700000 | tf_op jit(solution)/shard_map/ffn_back/pallas_call | solution.py:53
  87.0 8.2 %up_grads.1 = (f32[4,96,768]{2,1,0:T(8,128)}, f32[4,96,768]{2,1,0:T(8,128)}, bf16[4,96,768]{2,1,0:T(8,128)(2,1)}, bf16[4,96,768]{2,1,0:T(8,128)(2,1)}) custom-call(s32[1]{0:T(128)} %bitcast.11.place_ref.parity_ref, bf16[512,768]{1,0:T(8,128)(2,1)} %get-tuple-element.135.left_mine_ref, bf16[512,768]{1,0:T(8,128)(2,1)} %get-tuple-element.136.left_other_ref, ...), custom_call_target="tpu_custom_call" | custom-call | flops 200000000 | bytes 400000 | tf_op jit(solution)/shard_map/up_grads/pallas_call | solution.py:53
  95.3 8.3 %down_grads.1 = (f32[4,96,768]{2,1,0:T(8,128)}, f32[4,96,768]{2,1,0:T(8,128)}, bf16[4,96,768]{2,1,0:T(8,128)(2,1)}, bf16[4,96,768]{2,1,0:T(8,128)(2,1)}) custom-call(s32[1]{0:T(128)} %bitcast.10.place_ref, bf16[512,768]{1,0:T(8,128)(2,1)} %get-tuple-element.140.left_mine_ref, bf16[512,768]{1,0:T(8,128)(2,1)} %get-tuple-element.141.left_other_ref, ...), custom_call_target="tpu_custom_call" | custom-call | flops 200000000 | bytes 400000 | tf_op jit(solution)/shard_map/down_grads/pallas_call | solution.py:53
  103.7 3.8 %norm_one_back.1 = (f32[512,768]{1,0:T(8,128)}, bf16[536,768]{1,0:T(8,128)(2,1)}, f32[8,768]{1,0:T(8,128)S(1)}) custom-call(f32[512,768]{1,0:T(8,128)S(1)} %copy-done.15, f32[512,768]{1,0:T(8,128)S(1)} %copy-done.17, bf16[512,768]{1,0:T(8,128)(2,1)} %collective-permute-done.14.far_ref, f32[512,768]{1,0:T(8,128)S(1)} %copy-done.13, f32[512,1]{1,0:T(8,128)S(1)} %copy-done.26, ...), custom_call_target="tpu_custom_call" | custom-call | flops 55000000 | bytes 110000 | tf_op jit(solution)/shard_map/norm_one_back/pallas_call | solution.py:53
  113.7 12.7 %attend_backward.2 = (bf16[1024,576]{1,0:T(8,128)(2,1)}, f32[3,192]{1,0:T(4,128)S(1)}, f32[512,768]{1,0:T(8,128)}, bf16[512,768]{1,0:T(8,128)(2,1)}, f32[192,768]{1,0:T(8,128)}) custom-call(s32[1]{0:T(128)} %bitcast.1.core_ref, bf16[536,768]{1,0:T(8,128)(2,1)S(1)} %copy-done.8, bf16[536,768]{1,0:T(8,128)(2,1)S(1)} %collective-permute-done.15.second_ref.partner_ref, ...), custom_call_target="tpu_custom_call" | custom-call | flops 600000000 | bytes 1200000 | tf_op jit(solution)/shard_map/attend_backward/pallas_call | solution.py:53
  128.0 3.4 %combine.1 = bf16[8,96,768]{2,1,0:T(8,128)(2,1)} custom-call(f32[4,96,768]{2,1,0:T(8,128)} %get-tuple-element.158.up_ref, bf16[4,96,768]{2,1,0:T(8,128)(2,1)} %copy-done.57, f32[4,96,768]{2,1,0:T(8,128)} %get-tuple-element.161.down_ref, bf16[4,96,768]{2,1,0:T(8,128)(2,1)} %copy-done.58), custom_call_target="tpu_custom_call" | custom-call | flops 5000000000 | bytes 10000000 | tf_op jit(solution)/shard_map/combine/pallas_call | solution.py:53
  134.2 13.6 %attend_backward.3 = (bf16[1024,576]{1,0:T(8,128)(2,1)}, f32[3,192]{1,0:T(4,128)S(1)}, f32[512,768]{1,0:T(8,128)}, bf16[512,768]{1,0:T(8,128)(2,1)S(1)}, f32[192,768]{1,0:T(8,128)}) custom-call(s32[1]{0:T(128)} %bitcast.1.core_ref, bf16[536,768]{1,0:T(8,128)(2,1)S(1)} %collective-permute-done.19.first_ref.across_ref, ...), custom_call_target="tpu_custom_call" | custom-call | flops 600000000 | bytes 1200000 | tf_op jit(solution)/shard_map/attend_backward/pallas_call | solution.py:53
  148.4 10.3 %collective-permute-done.23.across_ref = bf16[8,96,768]{2,1,0:T(8,128)(2,1)S(1)} collective-permute-done((bf16[8,96,768]{2,1,0:T(8,128)(2,1)}, bf16[8,96,768]{2,1,0:T(8,128)(2,1)S(1)}, u32[]{:S(2)}, u32[]{:S(2)}) %collective-permute-start.23) | collective-permute-done | bytes 1179680 | tf_op jit(solution)/shard_map/ppermute | solution.py:620
  158.7 6.6 %qkv_pieces.1 = (f32[4,120,768]{2,1,0:T(8,128)}, bf16[4,120,768]{2,1,0:T(8,128)(2,1)}) custom-call(s32[1]{0:T(128)} %bitcast.2.place_ref, s32[1]{0:T(128)} %bitcast.11.place_ref.parity_ref, bf16[2048,768]{1,0:T(8,128)(2,1)S(1)} %copy-done.1, bf16[1024,576]{1,0:T(8,128)(2,1)} %get-tuple-element.159.near_ref, bf16[1024,576]{1,0:T(8,128)(2,1)} %get-tuple-element.175.far_ref, ...), custom_call_target="tpu_custom_call" | custom-call | flops 185000000 | bytes 370000 | tf_op jit(solution)/shard_map/qkv_pieces/pallas_call | solution.py:53
  168.6 2.6 %sum_far.1 = bf16[512,768]{1,0:T(8,128)(2,1)} custom-call(f32[512,768]{1,0:T(8,128)} %get-tuple-element.168.refs_0_, bf16[512,768]{1,0:T(8,128)(2,1)} %copy-done.33), custom_call_target="tpu_custom_call" | custom-call | flops 35000000 | bytes 70000 | tf_op jit(solution)/shard_map/sum_far/pallas_call | solution.py:53
  171.8 3.7 %split.1 = (bf16[96,768]{1,0:T(8,128)(2,1)}, bf16[96,768]{1,0:T(8,128)(2,1)}, bf16[96,768]{1,0:T(8,128)(2,1)}, bf16[96,768]{1,0:T(8,128)(2,1)}, bf16[96,768]{1,0...) custom-call(s32[2]{0:T(128)S(1)} %pad_add_fusion.members_ref, ...), custom_call_target="tpu_custom_call" | custom-call | flops 50000000 | bytes 100000 | tf_op jit(solution)/shard_map/split/pallas_call | solution.py:53
  176.7 2.6 %collective-permute-start.27 = (bf16[96,768]{1,0:T(8,128)(2,1)}, bf16[96,768]{1,0:T(8,128)(2,1)S(1)}, u32[]{:S(2)}, u32[]{:S(2)}) collective-permute-start(bf16[96,768]{1,0:T(8,128)(2,1)} %get-tuple-element.188), channel_id=1, source_target_pairs={{0,16},{4,20},{8,24},{12,28},{16,0},{20,4},{24,8},{28,12},{1,17},{... | collective-permute-start | bytes 442376 | tf_op jit(solution)/shard_map/ppermute | solution.py:625
  179.9 4.7 %collective-permute-done.32.received_ref = bf16[4,120,768]{2,1,0:T(8,128)(2,1)S(1)} collective-permute-done((bf16[4,120,768]{2,1,0:T(8,128)(2,1)}, bf16[4,120,768]{2,1,0:T(8,128)(2,1)S(1)}, u32[]{:S(2)}, u32[]{:S(2)}) %collective-permute-start.32) | collective-permute-done | bytes 737312 | tf_op jit(solution)/shard_map/ppermute | solution.py:625
  185.4 2.5 %qkv_split.1 = (bf16[120,768]{1,0:T(8,128)(2,1)}, bf16[120,768]{1,0:T(8,128)(2,1)}, bf16[120,768]{1,0:T(8,128)(2,1)}, bf16[120,768]{1,0:T(8,128)(2,1)}) custom-call(s32[2]{0:T(128)S(1)} %pad_add_fusion.members_ref, f32[4,120,768]{2,1,0:T(8,128)} %get-tuple-element.181.kept_ref, bf16[4,120,768]{2,1,0:T(8,128)(2,1)} %copy-done.34), custom_call_target="tpu_custom_call" | custom-call | flops 50000000 | bytes 100000 | tf_op jit(solution)/shard_map/qkv_split/pallas_call | solution.py:53
  193.4 3.1 %collective-permute-start.30 = (bf16[96,768]{1,0:T(8,128)(2,1)S(1)}, bf16[96,768]{1,0:T(8,128)(2,1)S(1)}, u32[]{:S(2)}, u32[]{:S(2)}) collective-permute-start(bf16[96,768]{1,0:T(8,128)(2,1)S(1)} %copy-done.60), channel_id=1, source_target_pairs={{0,16},{4,20},{8,24},{12,28},{16,0},{20,4},{24,8},{28,12},{1,17},{... | collective-permute-start | bytes 442376 | tf_op jit(solution)/shard_map/ppermute | solution.py:625
  197.8 3.7 %sum_in.1 = f32[512,768]{1,0:T(8,128)} custom-call(f32[512,768]{1,0:T(8,128)} %get-tuple-element.151.refs_0_, f32[512,768]{1,0:T(8,128)} %get-tuple-element.156.refs_1_, bf16[512,768]{1,0:T(8,128)(2,1)} %copy-done.31, bf16[512,768]{1,0:T(8,128)(2,1)} %copy-done.32), custom_call_target="tpu_custom_call" | custom-call | flops 50000000 | bytes 100000 | tf_op jit(solution)/shard_map/sum_in/pallas_call | solution.py:53
  201.5 18.0 %collective-permute-done.30.refs_6_ = bf16[96,768]{1,0:T(8,128)(2,1)S(1)} collective-permute-done((bf16[96,768]{1,0:T(8,128)(2,1)S(1)}, bf16[96,768]{1,0:T(8,128)(2,1)S(1)}, u32[]{:S(2)}, u32[]{:S(2)}) %collective-permute-start.30) | collective-permute-done | bytes 147488 | tf_op jit(solution)/shard_map/ppermute | solution.py:625
  219.5 2.5 %collective-permute-done.31.refs_7_ = bf16[96,768]{1,0:T(8,128)(2,1)S(1)} collective-permute-done((bf16[96,768]{1,0:T(8,128)(2,1)S(1)}, bf16[96,768]{1,0:T(8,128)(2,1)S(1)}, u32[]{:S(2)}, u32[]{:S(2)}) %collective-permute-start.31) | collective-permute-done | bytes 147488 | tf_op jit(solution)/shard_map/ppermute | solution.py:625
  222.9 2.6 %finish.1 = (f32[96,192]{1,0:T(8,128)}, f32[96,192]{1,0:T(8,128)}, f32[96,192]{1,0:T(8,128)}, f32[192,96]{1,0:T(8,128)}, f32[1,768]{1,0:T(1,128)S(1)}, /*index=5...) custom-call(bf16[96,768]{1,0:T(8,128)(2,1)} %get-tuple-element.186.refs_0_, bf16[96,768]{1,0:T(8,128)(2,1)} %copy-done.40, ...), custom_call_target="tpu_custom_call" | custom-call | flops 75000000 | bytes 150000 | tf_op jit(solution)/shard_map/finish/pallas_call | solution.py:53
  (201 shorter events, 45.4 us)
Async XLA Ops:
  1.7 11.0 %collective-permute-start = (bf16[192,768]{1,0:T(8,128)(2,1)S(1)}, bf16[192,768]{1,0:T(8,128)(2,1)}, u32[]{:S(2)}, u32[]{:S(2)}) collective-permute-start(bf16[192,768]{1,0:T(8,128)(2,1)S(1)} %constant_dynamic-slice_fusion.1), channel_id=1, source_target_pairs={{0,2},{1,3},{2,0},{3,1},{4,6},{5,7},{6,4},{7,5},{8,10},{9,11},{10,... | collective-permute-start | bytes 884744 | tf_op jit(solution)/shard_map/ppermute | solution.py:620
  6.4 25.9 %collective-permute-start.1 = (bf16[192,768]{1,0:T(8,128)(2,1)}, bf16[192,768]{1,0:T(8,128)(2,1)}, u32[]{:S(2)}, u32[]{:S(2)}) collective-permute-start(bf16[192,768]{1,0:T(8,128)(2,1)} %constant_dynamic-slice_fusion), channel_id=1, source_target_pairs={{0,2},{1,3},{2,0},{3,1},{4,6},{5,7},{6,4},{7,5},{8,10},{9,11},{10,... | collective-permute-start | bytes 884744 | tf_op jit(solution)/shard_map/ppermute | solution.py:620
  12.7 19.8 %collective-permute-start.4 = (bf16[192,768]{1,0:T(8,128)(2,1)}, bf16[192,768]{1,0:T(8,128)(2,1)}, u32[]{:S(2)}, u32[]{:S(2)}) collective-permute-start(bf16[192,768]{1,0:T(8,128)(2,1)} %collective-permute-done.refs_0_), channel_id=1, source_target_pairs={{0,12},{4,8},{8,4},{12,0},{16,28},{20,24},{24,20},{28,16},{1,13},{... | collective-permute-start | bytes 884744 | tf_op jit(solution)/shard_map/ppermute | solution.py:625
  15.7 19.6 %collective-permute-start.3 = (bf16[192,768]{1,0:T(8,128)(2,1)}, bf16[192,768]{1,0:T(8,128)(2,1)}, u32[]{:S(2)}, u32[]{:S(2)}) collective-permute-start(bf16[192,768]{1,0:T(8,128)(2,1)} %collective-permute-done.refs_0_), channel_id=1, source_target_pairs={{0,8},{4,12},{8,0},{12,4},{16,24},{20,28},{24,16},{28,20},{1,9},{5... | collective-permute-start | bytes 884744 | tf_op jit(solution)/shard_map/ppermute | solution.py:625
  16.2 19.6 %collective-permute-start.2 = (bf16[192,768]{1,0:T(8,128)(2,1)}, bf16[192,768]{1,0:T(8,128)(2,1)}, u32[]{:S(2)}, u32[]{:S(2)}) collective-permute-start(bf16[192,768]{1,0:T(8,128)(2,1)} %collective-permute-done.refs_0_), channel_id=1, source_target_pairs={{0,4},{4,0},{8,12},{12,8},{16,20},{20,16},{24,28},{28,24},{1,5},{5... | collective-permute-start | bytes 884744 | tf_op jit(solution)/shard_map/ppermute | solution.py:625
  29.6 18.2 %collective-permute-start.8 = (bf16[1024,192]{1,0:T(8,128)(2,1)}, bf16[1024,192]{1,0:T(8,128)(2,1)}, u32[]{:S(2)}, u32[]{:S(2)}) collective-permute-start(bf16[1024,192]{1,0:T(8,128)(2,1)} %get-tuple-element.113.context_ref), channel_id=1, source_target_pairs={{0,2},{1,3},{2,0},{3,1},{4,6},{5,7},{6,4},{7,5},{8,10},{9,11},{10,... | collective-permute-start | bytes 1179656 | tf_op jit(solution)/shard_map/ppermute | solution.py:620
  32.3 15.5 %collective-permute-start.9 = (bf16[200,768]{1,0:T(8,128)(2,1)}, bf16[200,768]{1,0:T(8,128)(2,1)}, u32[]{:S(2)}, u32[]{:S(2)}) collective-permute-start(bf16[200,768]{1,0:T(8,128)(2,1)} %pad_maximum_fusion), channel_id=1, source_target_pairs={{0,2},{1,3},{2,0},{3,1},{4,6},{5,7},{6,4},{7,5},{8,10},{9,11},{10,... | collective-permute-start | bytes 921608 | tf_op jit(solution)/shard_map/ppermute | solution.py:620
  32.4 13.9 %collective-permute-start.7 = (bf16[192,768]{1,0:T(8,128)(2,1)}, bf16[192,768]{1,0:T(8,128)(2,1)}, u32[]{:S(2)}, u32[]{:S(2)}) collective-permute-start(bf16[192,768]{1,0:T(8,128)(2,1)} %collective-permute-done.1.refs_0_), channel_id=1, source_target_pairs={{0,12},{4,8},{8,4},{12,0},{16,28},{20,24},{24,20},{28,16},{1,13},{... | collective-permute-start | bytes 884744 | tf_op jit(solution)/shard_map/ppermute | solution.py:625
  35.3 11.0 %collective-permute-start.6 = (bf16[192,768]{1,0:T(8,128)(2,1)}, bf16[192,768]{1,0:T(8,128)(2,1)}, u32[]{:S(2)}, u32[]{:S(2)}) collective-permute-start(bf16[192,768]{1,0:T(8,128)(2,1)} %collective-permute-done.1.refs_0_), channel_id=1, source_target_pairs={{0,8},{4,12},{8,0},{12,4},{16,24},{20,28},{24,16},{28,20},{1,9},{5... | collective-permute-start | bytes 884744 | tf_op jit(solution)/shard_map/ppermute | solution.py:625
  35.8 10.6 %collective-permute-start.5 = (bf16[192,768]{1,0:T(8,128)(2,1)}, bf16[192,768]{1,0:T(8,128)(2,1)}, u32[]{:S(2)}, u32[]{:S(2)}) collective-permute-start(bf16[192,768]{1,0:T(8,128)(2,1)} %collective-permute-done.1.refs_0_), channel_id=1, source_target_pairs={{0,4},{4,0},{8,12},{12,8},{16,20},{20,16},{24,28},{28,24},{1,5},{5... | collective-permute-start | bytes 884744 | tf_op jit(solution)/shard_map/ppermute | solution.py:625
  70.1 2.4 %collective-permute-start.12 = (bf16[512,768]{1,0:T(8,128)(2,1)S(1)}, bf16[512,768]{1,0:T(8,128)(2,1)S(1)}, u32[]{:S(2)}, u32[]{:S(2)}) collective-permute-start(bf16[512,768]{1,0:T(8,128)(2,1)S(1)} %get-tuple-element.125), channel_id=1, source_target_pairs={{0,1},{1,0},{2,3},{3,2},{4,5},{5,4},{6,7},{7,6},{8,9},{9,8},{10,11... | collective-permute-start | bytes 2359304 | tf_op jit(solution)/shard_map/ppermute | solution.py:620
  86.9 16.7 %collective-permute-start.14 = (bf16[512,768]{1,0:T(8,128)(2,1)}, bf16[512,768]{1,0:T(8,128)(2,1)}, u32[]{:S(2)}, u32[]{:S(2)}) collective-permute-start(bf16[512,768]{1,0:T(8,128)(2,1)} %get-tuple-element.146), channel_id=1, source_target_pairs={{0,1},{1,0},{2,3},{3,2},{4,5},{5,4},{6,7},{7,6},{8,9},{9,8},{10,11... | collective-permute-start | bytes 2359304 | tf_op jit(solution)/shard_map/ppermute | solution.py:620
  107.5 4.9 %collective-permute-start.15 = (bf16[536,768]{1,0:T(8,128)(2,1)}, bf16[536,768]{1,0:T(8,128)(2,1)S(1)}, u32[]{:S(2)}, u32[]{:S(2)}) collective-permute-start(bf16[536,768]{1,0:T(8,128)(2,1)} %get-tuple-element.152.first_ref.mine_ref), channel_id=1, source_target_pairs={{0,1},{1,0},{2,3},{3,2},{4,5},{5,4},{6,7},{7,6},{8,9},{9,8},{10,11... | collective-permute-start | bytes 2469896 | tf_op jit(solution)/shard_map/ppermute | solution.py:620
  107.9 19.0 %collective-permute-start.16 = (bf16[4,96,768]{2,1,0:T(8,128)(2,1)S(1)}, bf16[4,96,768]{2,1,0:T(8,128)(2,1)S(1)}, u32[]{:S(2)}, u32[]{:S(2)}) collective-permute-start(bf16[4,96,768]{2,1,0:T(8,128)(2,1)S(1)} %copy-done.55), channel_id=1, source_target_pairs={{0,4},{4,0},{8,12},{12,8},{16,20},{20,16},{24,28},{28,24},{1,5},{5... | collective-permute-start | bytes 1769480 | tf_op jit(solution)/shard_map/ppermute | solution.py:625
  109.4 17.5 %collective-permute-start.17 = (bf16[4,96,768]{2,1,0:T(8,128)(2,1)S(1)}, bf16[4,96,768]{2,1,0:T(8,128)(2,1)S(1)}, u32[]{:S(2)}, u32[]{:S(2)}) collective-permute-start(bf16[4,96,768]{2,1,0:T(8,128)(2,1)S(1)} %copy-done.56), channel_id=1, source_target_pairs={{0,8},{4,12},{8,0},{12,4},{16,24},{20,28},{24,16},{28,20},{1,9},{5... | collective-permute-start | bytes 1769480 | tf_op jit(solution)/shard_map/ppermute | solution.py:625
  111.0 20.9 %collective-permute-start.19 = (bf16[536,768]{1,0:T(8,128)(2,1)}, bf16[536,768]{1,0:T(8,128)(2,1)S(1)}, u32[]{:S(2)}, u32[]{:S(2)}) collective-permute-start(bf16[536,768]{1,0:T(8,128)(2,1)} %get-tuple-element.152.first_ref.mine_ref), channel_id=1, source_target_pairs={{0,2},{1,3},{2,0},{3,1},{4,6},{5,7},{6,4},{7,5},{8,10},{9,11},{10,... | collective-permute-start | bytes 2469896 | tf_op jit(solution)/shard_map/ppermute | solution.py:620
  131.3 27.4 %collective-permute-start.23 = (bf16[8,96,768]{2,1,0:T(8,128)(2,1)}, bf16[8,96,768]{2,1,0:T(8,128)(2,1)S(1)}, u32[]{:S(2)}, u32[]{:S(2)}) collective-permute-start(bf16[8,96,768]{2,1,0:T(8,128)(2,1)} %combine.1), channel_id=1, source_target_pairs={{0,2},{1,3},{2,0},{3,1},{4,6},{5,7},{6,4},{7,5},{8,10},{9,11},{10,... | collective-permute-start | bytes 3538952 | tf_op jit(solution)/shard_map/ppermute | solution.py:620
  131.9 16.5 %collective-permute-start.21 = (bf16[4,96,768]{2,1,0:T(8,128)(2,1)S(1)}, bf16[4,96,768]{2,1,0:T(8,128)(2,1)S(1)}, u32[]{:S(2)}, u32[]{:S(2)}) collective-permute-start(bf16[4,96,768]{2,1,0:T(8,128)(2,1)S(1)} %copy-done.53), channel_id=1, source_target_pairs={{0,4},{4,0},{8,12},{12,8},{16,20},{20,16},{24,28},{28,24},{1,5},{5... | collective-permute-start | bytes 1769480 | tf_op jit(solution)/shard_map/ppermute | solution.py:625
  132.5 15.9 %collective-permute-start.22 = (bf16[4,96,768]{2,1,0:T(8,128)(2,1)S(1)}, bf16[4,96,768]{2,1,0:T(8,128)(2,1)S(1)}, u32[]{:S(2)}, u32[]{:S(2)}) collective-permute-start(bf16[4,96,768]{2,1,0:T(8,128)(2,1)S(1)} %copy-done.54), channel_id=1, source_target_pairs={{0,8},{4,12},{8,0},{12,4},{16,24},{20,28},{24,16},{28,20},{1,9},{5... | collective-permute-start | bytes 1769480 | tf_op jit(solution)/shard_map/ppermute | solution.py:625
  165.3 2.4 %collective-permute-start.24 = (bf16[512,768]{1,0:T(8,128)(2,1)S(1)}, bf16[512,768]{1,0:T(8,128)(2,1)S(1)}, u32[]{:S(2)}, u32[]{:S(2)}) collective-permute-start(bf16[512,768]{1,0:T(8,128)(2,1)S(1)} %get-tuple-element.182), channel_id=1, source_target_pairs={{0,1},{1,0},{2,3},{3,2},{4,5},{5,4},{6,7},{7,6},{8,9},{9,8},{10,11... | collective-permute-start | bytes 2359304 | tf_op jit(solution)/shard_map/ppermute | solution.py:620
  165.4 13.9 %collective-permute-start.18 = (bf16[512,768]{1,0:T(8,128)(2,1)}, bf16[512,768]{1,0:T(8,128)(2,1)S(1)}, u32[]{:S(2)}, u32[]{:S(2)}) collective-permute-start(bf16[512,768]{1,0:T(8,128)(2,1)} %get-tuple-element.162), channel_id=1, source_target_pairs={{0,1},{1,0},{2,3},{3,2},{4,5},{5,4},{6,7},{7,6},{8,9},{9,8},{10,11... | collective-permute-start | bytes 2359304 | tf_op jit(solution)/shard_map/ppermute | solution.py:620
  165.9 18.7 %collective-permute-start.32 = (bf16[4,120,768]{2,1,0:T(8,128)(2,1)}, bf16[4,120,768]{2,1,0:T(8,128)(2,1)S(1)}, u32[]{:S(2)}, u32[]{:S(2)}) collective-permute-start(bf16[4,120,768]{2,1,0:T(8,128)(2,1)} %get-tuple-element.194), channel_id=1, source_target_pairs={{0,4},{4,0},{8,12},{12,8},{16,20},{20,16},{24,28},{28,24},{1,5},{5... | collective-permute-start | bytes 2211848 | tf_op jit(solution)/shard_map/ppermute | solution.py:625
  171.2 25.3 %collective-permute-start.25 = (bf16[512,768]{1,0:T(8,128)(2,1)}, bf16[512,768]{1,0:T(8,128)(2,1)S(1)}, u32[]{:S(2)}, u32[]{:S(2)}) collective-permute-start(bf16[512,768]{1,0:T(8,128)(2,1)} %sum_far.1), channel_id=1, source_target_pairs={{0,2},{1,3},{2,0},{3,1},{4,6},{5,7},{6,4},{7,5},{8,10},{9,11},{10,... | collective-permute-start | bytes 2359304 | tf_op jit(solution)/shard_map/ppermute | solution.py:620
  175.5 12.5 %collective-permute-start.26 = (bf16[96,768]{1,0:T(8,128)(2,1)}, bf16[96,768]{1,0:T(8,128)(2,1)S(1)}, u32[]{:S(2)}, u32[]{:S(2)}) collective-permute-start(bf16[96,768]{1,0:T(8,128)(2,1)} %get-tuple-element.187), channel_id=1, source_target_pairs={{0,8},{4,12},{8,0},{12,4},{16,24},{20,28},{24,16},{28,20},{1,9},{5... | collective-permute-start | bytes 442376 | tf_op jit(solution)/shard_map/ppermute | solution.py:625
  176.7 14.2 %collective-permute-start.27 = (bf16[96,768]{1,0:T(8,128)(2,1)}, bf16[96,768]{1,0:T(8,128)(2,1)S(1)}, u32[]{:S(2)}, u32[]{:S(2)}) collective-permute-start(bf16[96,768]{1,0:T(8,128)(2,1)} %get-tuple-element.188), channel_id=1, source_target_pairs={{0,16},{4,20},{8,24},{12,28},{16,0},{20,4},{24,8},{28,12},{1,17},{... | collective-permute-start | bytes 442376 | tf_op jit(solution)/shard_map/ppermute | solution.py:625
  179.3 12.2 %collective-permute-start.28 = (bf16[96,768]{1,0:T(8,128)(2,1)}, bf16[96,768]{1,0:T(8,128)(2,1)S(1)}, u32[]{:S(2)}, u32[]{:S(2)}) collective-permute-start(bf16[96,768]{1,0:T(8,128)(2,1)} %get-tuple-element.189), channel_id=1, source_target_pairs={{0,24},{4,28},{8,16},{12,20},{16,8},{20,12},{24,0},{28,4},{1,25},{... | collective-permute-start | bytes 442376 | tf_op jit(solution)/shard_map/ppermute | solution.py:625
  184.6 8.8 %collective-permute-start.29 = (bf16[96,768]{1,0:T(8,128)(2,1)}, bf16[96,768]{1,0:T(8,128)(2,1)S(1)}, u32[]{:S(2)}, u32[]{:S(2)}) collective-permute-start(bf16[96,768]{1,0:T(8,128)(2,1)} %get-tuple-element.191), channel_id=1, source_target_pairs={{0,4},{4,0},{8,12},{12,8},{16,20},{20,16},{24,28},{28,24},{1,5},{5... | collective-permute-start | bytes 442376 | tf_op jit(solution)/shard_map/ppermute | solution.py:625
  187.9 34.1 %collective-permute-start.33 = (bf16[120,768]{1,0:T(8,128)(2,1)}, bf16[120,768]{1,0:T(8,128)(2,1)S(1)}, u32[]{:S(2)}, u32[]{:S(2)}) collective-permute-start(bf16[120,768]{1,0:T(8,128)(2,1)} %get-tuple-element.196), channel_id=1, source_target_pairs={{0,8},{4,12},{8,0},{12,4},{16,24},{20,28},{24,16},{28,20},{1,9},{5... | collective-permute-start | bytes 552968 | tf_op jit(solution)/shard_map/ppermute | solution.py:625
  190.9 31.2 %collective-permute-start.34 = (bf16[120,768]{1,0:T(8,128)(2,1)}, bf16[120,768]{1,0:T(8,128)(2,1)S(1)}, u32[]{:S(2)}, u32[]{:S(2)}) collective-permute-start(bf16[120,768]{1,0:T(8,128)(2,1)} %get-tuple-element.197), channel_id=1, source_target_pairs={{0,16},{4,20},{8,24},{12,28},{16,0},{20,4},{24,8},{28,12},{1,17},{... | collective-permute-start | bytes 552968 | tf_op jit(solution)/shard_map/ppermute | solution.py:625
  191.5 30.6 %collective-permute-start.35 = (bf16[120,768]{1,0:T(8,128)(2,1)}, bf16[120,768]{1,0:T(8,128)(2,1)S(1)}, u32[]{:S(2)}, u32[]{:S(2)}) collective-permute-start(bf16[120,768]{1,0:T(8,128)(2,1)} %get-tuple-element.198), channel_id=1, source_target_pairs={{0,24},{4,28},{8,16},{12,20},{16,8},{20,12},{24,0},{28,4},{1,25},{... | collective-permute-start | bytes 552968 | tf_op jit(solution)/shard_map/ppermute | solution.py:625
  193.4 26.1 %collective-permute-start.30 = (bf16[96,768]{1,0:T(8,128)(2,1)S(1)}, bf16[96,768]{1,0:T(8,128)(2,1)S(1)}, u32[]{:S(2)}, u32[]{:S(2)}) collective-permute-start(bf16[96,768]{1,0:T(8,128)(2,1)S(1)} %copy-done.60), channel_id=1, source_target_pairs={{0,16},{4,20},{8,24},{12,28},{16,0},{20,4},{24,8},{28,12},{1,17},{... | collective-permute-start | bytes 442376 | tf_op jit(solution)/shard_map/ppermute | solution.py:625
  196.5 25.6 %collective-permute-start.31 = (bf16[96,768]{1,0:T(8,128)(2,1)S(1)}, bf16[96,768]{1,0:T(8,128)(2,1)S(1)}, u32[]{:S(2)}, u32[]{:S(2)}) collective-permute-start(bf16[96,768]{1,0:T(8,128)(2,1)S(1)} %copy-done.59), channel_id=1, source_target_pairs={{0,20},{4,16},{8,28},{12,24},{16,4},{20,0},{24,12},{28,8},{1,21},{... | collective-permute-start | bytes 442376 | tf_op jit(solution)/shard_map/ppermute | solution.py:625
  (65 other events, 538.9 us)
where the time goes:
time: 227 us
  Pallas kernels  121 us (53%)
  waiting for transfers between devices  55.6 us (24%)
  starting transfers between devices  34.6 us (15%)
  local copies, waits for them, and re-layouts  12.5 us (6%)
    pallas_call x21, Pallas kernels, call(): pl.pallas_call(kernel, out_shape=tuple((pltpu.HBM(*out[:2]) if len(out) >...  121 us
    ppermute x16, waiting for transfers between devices, swap_tensor(): return lax.ppermute(array, 'tensor', [(i, i ^ mask) for i in range(ways)])  28.4 us
    ppermute x20, waiting for transfers between devices, swap_dp(): return lax.ppermute(array, 'dp', [(i, i ^ mask) for i in range(ways)])  27.2 us
    ppermute x20, starting transfers between devices, swap_dp(): return lax.ppermute(array, 'dp', [(i, i ^ mask) for i in range(ways)])  25.3 us
    ppermute x16, starting transfers between devices, swap_tensor(): return lax.ppermute(array, 'tensor', [(i, i ^ mask) for i in range(ways)])  9.28 us
    unnamed x122, local copies, waits for them, and re-layouts  8.58 us
  transfers between devices with their start and end apart: 36, of which 13 were waited for; matrix products, arithmetic and copies ran while one was open for 1% of the time, Pallas kernels for 35%

commit v1 on v0

--- a/solution.py
+++ b/solution.py
@@ -26,6 +26,7 @@
 TILE = 256
 SUMS = 8
 ROWS = 128
+WIDE = 384
 HELD = True
 
 
@@ -480,13 +481,13 @@
         (mine_ref, kept_mine_ref, sent_mine_ref), (other_ref, kept_other_ref, sent_other_ref)
     ):
         def block(begin, carry, right_ref=right_ref):
-            columns = pl.ds(begin, TILE)
+            columns = pl.ds(begin, WIDE)
             whole_s[columns] = tn(left_mine_ref[:, columns], right_ref[:half]) + tn(
                 left_other_ref[:, columns], right_ref[half:]
             )
             return carry
 
-        over_rows(whole_s.shape[0], TILE, block, 0)
+        over_rows(whole_s.shape[0], WIDE, block, 0)
         for member in range(count):
             base = member % bit + member // bit * 2 * bit
             for parity, made_ref in ((own, kept_ref), (1 - own, sent_ref)):

time: 227 us -> 227 us (level)
  no operation moved by 1% of the time
where the time goes in v1:
time: 227 us; the launch traced here: 226 us
  Pallas kernels  121 us (53%)
  waiting for transfers between devices  55.6 us (24%)
  starting transfers between devices  34.5 us (15%)
  local copies, waits for them, and re-layouts  12.5 us (6%)
    pallas_call x21, Pallas kernels, call(): pl.pallas_call(kernel, out_shape=tuple((pltpu.HBM(*out[:2]) if len(out) >...  121 us
    ppermute x16, waiting for transfers between devices, swap_tensor(): return lax.ppermute(array, 'tensor', [(i, i ^ mask) for i in range(ways)])  28.4 us
    ppermute x20, waiting for transfers between devices, swap_dp(): return lax.ppermute(array, 'dp', [(i, i ^ mask) for i in range(ways)])  27.2 us
    ppermute x20, starting transfers between devices, swap_dp(): return lax.ppermute(array, 'dp', [(i, i ^ mask) for i in range(ways)])  25.2 us
    ppermute x16, starting transfers between devices, swap_tensor(): return lax.ppermute(array, 'tensor', [(i, i ^ mask) for i in range(ways)])  9.29 us
    unnamed x122, local copies, waits for them, and re-layouts  8.59 us
  transfers between devices with their start and end apart: 36, of which 13 were waited for; matrix products, arithmetic and copies ran while one was open for 1% of the time, Pallas kernels for 35%

profile of v1, /device:TPU:0, one launch (start us, length us, event | category | flops | bytes accessed | tf_op | source)
XLA Modules:
  0.0 226.2 jit_solution(10531571474027325876)
XLA Ops:
  1.7 3.0 %collective-permute-start = (bf16[192,768]{1,0:T(8,128)(2,1)S(1)}, bf16[192,768]{1,0:T(8,128)(2,1)}, u32[]{:S(2)}, u32[]{:S(2)}) collective-permute-start(bf16[192,768]{1,0:T(8,128)(2,1)S(1)} %constant_dynamic-slice_fusion.1), channel_id=1, source_target_pairs={{0,2},{1,3},{2,0},{3,1},{4,6},{5,7},{6,4},{7,5},{8,10},{9,11},{10,... | collective-permute-start | bytes 884744 | tf_op jit(solution)/shard_map/ppermute | solution.py:621
  6.4 6.2 %collective-permute-done.refs_0_ = bf16[192,768]{1,0:T(8,128)(2,1)} collective-permute-done((bf16[192,768]{1,0:T(8,128)(2,1)S(1)}, bf16[192,768]{1,0:T(8,128)(2,1)}, u32[]{:S(2)}, u32[]{:S(2)}) %collective-permute-start) | collective-permute-done | bytes 294944 | tf_op jit(solution)/shard_map/ppermute | solution.py:621
  12.7 3.1 %collective-permute-start.4 = (bf16[192,768]{1,0:T(8,128)(2,1)}, bf16[192,768]{1,0:T(8,128)(2,1)}, u32[]{:S(2)}, u32[]{:S(2)}) collective-permute-start(bf16[192,768]{1,0:T(8,128)(2,1)} %collective-permute-done.refs_0_), channel_id=1, source_target_pairs={{0,12},{4,8},{8,4},{12,0},{16,28},{20,24},{24,20},{28,16},{1,13},{... | collective-permute-start | bytes 884744 | tf_op jit(solution)/shard_map/ppermute | solution.py:626
  18.9 10.7 %attend_forward.2 = (bf16[1024,192]{1,0:T(8,128)(2,1)}, bf16[3,1024,128]{2,1,0:T(8,128)(2,1)}, bf16[3,1024,128]{2,1,0:T(8,128)(2,1)}, bf16[3,1024,128]{2,1,0:T(8,128)(2,1)}) custom-call(s32[1]{0:T(128)} %bitcast.3.place_ref, bf16[2048,768]{1,0:T(8,128)(2,1)S(1)} %copy-done, bf16[192,768]{1,0:T(8,128)(2,1)} %bitcast.17, bf16[192,768]{1,0:T(8,128)(2,1)} %bitcast.21, ...), custom_call_target="tpu_custom_call" | custom-call | flops 400000000 | bytes 800000 | tf_op jit(solution)/shard_map/attend_forward/pallas_call | solution.py:54
  32.4 2.9 %collective-permute-start.7 = (bf16[192,768]{1,0:T(8,128)(2,1)}, bf16[192,768]{1,0:T(8,128)(2,1)}, u32[]{:S(2)}, u32[]{:S(2)}) collective-permute-start(bf16[192,768]{1,0:T(8,128)(2,1)} %collective-permute-done.1.refs_0_), channel_id=1, source_target_pairs={{0,12},{4,8},{8,4},{12,0},{16,28},{20,24},{24,20},{28,16},{1,13},{... | collective-permute-start | bytes 884744 | tf_op jit(solution)/shard_map/ppermute | solution.py:626
  36.0 10.3 %attend_forward.3 = (bf16[1024,192]{1,0:T(8,128)(2,1)S(1)}, bf16[3,1024,128]{2,1,0:T(8,128)(2,1)}, bf16[3,1024,128]{2,1,0:T(8,128)(2,1)}, bf16[3,1024,128]{2,1,0:T(8,128)(2,1)}) custom-call(s32[1]{0:T(128)} %bitcast.2.place_ref, bf16[2048,768]{1,0:T(8,128)(2,1)S(1)} %copy-done.1, bf16[192,768]{1,0:T(8,128)(2,1)} %bitcast.18, bf16[192,768]{1,0:T(8,128)(2,1)} %bitcast.22, ...), custom_call_target="tpu_custom_call" | custom-call | flops 400000000 | bytes 800000 | tf_op jit(solution)/shard_map/attend_forward/pallas_call | solution.py:54
  50.0 2.2 collective-permute-done.10.far_ref
  54.4 2.1 collective-permute-done.11.other_ref
  56.5 3.8 %rise_mine.1 = (bf16[1024,768]{1,0:T(8,128)(2,1)S(1)}, bf16[1024,768]{1,0:T(8,128)(2,1)}, f32[1024,768]{1,0:T(8,128)S(1)}, bf16[512,768]{1,0:T(8,128)(2,1)}) custom-call(bf16[512,768]{1,0:T(8,128)(2,1)S(1)} %get-tuple-element.122.mine_ref, bf16[512,768]{1,0:T(8,128)(2,1)S(1)} %collective-permute-done.11.other_ref, bf16[768,768]{1,0:T(8,128)(2,1)S(1)} %copy-done.2, ...), custom_call_target="tpu_custom_call" | custom-call | flops 130000000 | bytes 260000 | tf_op jit(solution)/shard_map/rise_mine/pallas_call | solution.py:54
  60.3 5.3 %rise_other.1 = (bf16[1024,768]{1,0:T(8,128)(2,1)S(1)}, bf16[1024,768]{1,0:T(8,128)(2,1)}, f32[1024,768]{1,0:T(8,128)S(1)}, bf16[768,768]{1,0:T(8,128)(2,1)S(1)}) custom-call(s32[1]{0:T(128)} %bitcast.9.order_ref, bf16[512,768]{1,0:T(8,128)(2,1)S(1)} %get-tuple-element.122.mine_ref, bf16[512,768]{1,0:T(8,128)(2,1)S(1)} %collective-permute-done.11.other_ref, ...), custom_call_target="tpu_custom_call" | custom-call | flops 200000000 | bytes 400000 | tf_op jit(solution)/shard_map/rise_other/pallas_call | solution.py:54
  65.6 4.5 %fall.1 = (f32[512,768]{1,0:T(8,128)S(1)}, bf16[512,768]{1,0:T(8,128)(2,1)S(1)}, bf16[768,768]{1,0:T(8,128)(2,1)S(1)}) custom-call(s32[1]{0:T(128)} %bitcast.9.order_ref, bf16[1024,768]{1,0:T(8,128)(2,1)S(1)} %get-tuple-element.121.mine_ref, bf16[1024,768]{1,0:T(8,128)(2,1)S(1)} %get-tuple-element.123.other_ref, bf16[768,768]{1,0:T(8,128)(2,1)S(1)} %copy-done.3, ...), custom_call_target="tpu_custom_call" | custom-call | flops 135000000 | bytes 270000 | tf_op jit(solution)/shard_map/fall/pallas_call | solution.py:54
  72.5 2.7 %norm_two.1 = (bf16[512,768]{1,0:T(8,128)(2,1)}, f32[512,768]{1,0:T(8,128)S(1)}, bf16[512,768]{1,0:T(8,128)(2,1)S(1)}, bf16[512,768]{1,0:T(8,128)(2,1)}, f32[8,768]{1,0:T(8,128)S(1)}) custom-call(f32[512,768]{1,0:T(8,128)S(1)} %get-tuple-element.119.hidden_ref, f32[512,768]{1,0:T(8,128)S(1)} %get-tuple-element.124.near_ref, ...), custom_call_target="tpu_custom_call" | custom-call | flops 75000000 | bytes 150000 | tf_op jit(solution)/shard_map/norm_two/pallas_call | solution.py:54
  75.3 2.1 collective-permute-done.13.other_ref
  77.5 8.3 %ffn_back.1 = (bf16[1024,768]{1,0:T(8,128)(2,1)}, bf16[1024,768]{1,0:T(8,128)(2,1)}, f32[512,768]{1,0:T(8,128)S(1)}, bf16[512,768]{1,0:T(8,128)(2,1)}, f32[8,768]{1,0:T(8,128)S(1)}, /*index=5*/bf16[512,768]{1,0:T(8,128)(2,1)}) custom-call(bf16[512,768]{1,0:T(8,128)(2,1)S(1)} %get-tuple-element.128.mine_ref, ...), custom_call_target="tpu_custom_call" | custom-call | flops 350000000 | bytes 700000 | tf_op jit(solution)/shard_map/ffn_back/pallas_call | solution.py:54
  87.0 7.8 %up_grads.1 = (f32[4,96,768]{2,1,0:T(8,128)}, f32[4,96,768]{2,1,0:T(8,128)}, bf16[4,96,768]{2,1,0:T(8,128)(2,1)}, bf16[4,96,768]{2,1,0:T(8,128)(2,1)}) custom-call(s32[1]{0:T(128)} %bitcast.11.place_ref.parity_ref, bf16[512,768]{1,0:T(8,128)(2,1)} %get-tuple-element.135.left_mine_ref, bf16[512,768]{1,0:T(8,128)(2,1)} %get-tuple-element.136.left_other_ref, ...), custom_call_target="tpu_custom_call" | custom-call | flops 200000000 | bytes 400000 | tf_op jit(solution)/shard_map/up_grads/pallas_call | solution.py:54
  94.9 7.9 %down_grads.1 = (f32[4,96,768]{2,1,0:T(8,128)}, f32[4,96,768]{2,1,0:T(8,128)}, bf16[4,96,768]{2,1,0:T(8,128)(2,1)}, bf16[4,96,768]{2,1,0:T(8,128)(2,1)}) custom-call(s32[1]{0:T(128)} %bitcast.10.place_ref, bf16[512,768]{1,0:T(8,128)(2,1)} %get-tuple-element.140.left_mine_ref, bf16[512,768]{1,0:T(8,128)(2,1)} %get-tuple-element.141.left_other_ref, ...), custom_call_target="tpu_custom_call" | custom-call | flops 200000000 | bytes 400000 | tf_op jit(solution)/shard_map/down_grads/pallas_call | solution.py:54
  102.9 3.8 %norm_one_back.1 = (f32[512,768]{1,0:T(8,128)}, bf16[536,768]{1,0:T(8,128)(2,1)}, f32[8,768]{1,0:T(8,128)S(1)}) custom-call(f32[512,768]{1,0:T(8,128)S(1)} %copy-done.15, f32[512,768]{1,0:T(8,128)S(1)} %copy-done.17, bf16[512,768]{1,0:T(8,128)(2,1)} %collective-permute-done.14.far_ref, f32[512,768]{1,0:T(8,128)S(1)} %copy-done.13, f32[512,1]{1,0:T(8,128)S(1)} %copy-done.26, ...), custom_call_target="tpu_custom_call" | custom-call | flops 55000000 | bytes 110000 | tf_op jit(solution)/shard_map/norm_one_back/pallas_call | solution.py:54
  112.8 12.9 %attend_backward.2 = (bf16[1024,576]{1,0:T(8,128)(2,1)}, f32[3,192]{1,0:T(4,128)S(1)}, f32[512,768]{1,0:T(8,128)}, bf16[512,768]{1,0:T(8,128)(2,1)}, f32[192,768]{1,0:T(8,128)}) custom-call(s32[1]{0:T(128)} %bitcast.1.core_ref, bf16[536,768]{1,0:T(8,128)(2,1)S(1)} %copy-done.8, bf16[536,768]{1,0:T(8,128)(2,1)S(1)} %collective-permute-done.15.second_ref.partner_ref, ...), custom_call_target="tpu_custom_call" | custom-call | flops 600000000 | bytes 1200000 | tf_op jit(solution)/shard_map/attend_backward/pallas_call | solution.py:54
  127.4 3.4 %combine.1 = bf16[8,96,768]{2,1,0:T(8,128)(2,1)} custom-call(f32[4,96,768]{2,1,0:T(8,128)} %get-tuple-element.158.up_ref, bf16[4,96,768]{2,1,0:T(8,128)(2,1)} %copy-done.57, f32[4,96,768]{2,1,0:T(8,128)} %get-tuple-element.161.down_ref, bf16[4,96,768]{2,1,0:T(8,128)(2,1)} %copy-done.58), custom_call_target="tpu_custom_call" | custom-call | flops 5000000000 | bytes 10000000 | tf_op jit(solution)/shard_map/combine/pallas_call | solution.py:54
  133.6 13.6 %attend_backward.3 = (bf16[1024,576]{1,0:T(8,128)(2,1)}, f32[3,192]{1,0:T(4,128)S(1)}, f32[512,768]{1,0:T(8,128)}, bf16[512,768]{1,0:T(8,128)(2,1)S(1)}, f32[192,768]{1,0:T(8,128)}) custom-call(s32[1]{0:T(128)} %bitcast.1.core_ref, bf16[536,768]{1,0:T(8,128)(2,1)S(1)} %collective-permute-done.19.first_ref.across_ref, ...), custom_call_target="tpu_custom_call" | custom-call | flops 600000000 | bytes 1200000 | tf_op jit(solution)/shard_map/attend_backward/pallas_call | solution.py:54
  147.9 10.2 %collective-permute-done.23.across_ref = bf16[8,96,768]{2,1,0:T(8,128)(2,1)S(1)} collective-permute-done((bf16[8,96,768]{2,1,0:T(8,128)(2,1)}, bf16[8,96,768]{2,1,0:T(8,128)(2,1)S(1)}, u32[]{:S(2)}, u32[]{:S(2)}) %collective-permute-start.23) | collective-permute-done | bytes 1179680 | tf_op jit(solution)/shard_map/ppermute | solution.py:621
  158.1 6.6 %qkv_pieces.1 = (f32[4,120,768]{2,1,0:T(8,128)}, bf16[4,120,768]{2,1,0:T(8,128)(2,1)}) custom-call(s32[1]{0:T(128)} %bitcast.2.place_ref, s32[1]{0:T(128)} %bitcast.11.place_ref.parity_ref, bf16[2048,768]{1,0:T(8,128)(2,1)S(1)} %copy-done.1, bf16[1024,576]{1,0:T(8,128)(2,1)} %get-tuple-element.159.near_ref, bf16[1024,576]{1,0:T(8,128)(2,1)} %get-tuple-element.175.far_ref, ...), custom_call_target="tpu_custom_call" | custom-call | flops 185000000 | bytes 370000 | tf_op jit(solution)/shard_map/qkv_pieces/pallas_call | solution.py:54
  168.0 2.6 %sum_far.1 = bf16[512,768]{1,0:T(8,128)(2,1)} custom-call(f32[512,768]{1,0:T(8,128)} %get-tuple-element.168.refs_0_, bf16[512,768]{1,0:T(8,128)(2,1)} %copy-done.33), custom_call_target="tpu_custom_call" | custom-call | flops 35000000 | bytes 70000 | tf_op jit(solution)/shard_map/sum_far/pallas_call | solution.py:54
  171.2 3.7 %split.1 = (bf16[96,768]{1,0:T(8,128)(2,1)}, bf16[96,768]{1,0:T(8,128)(2,1)}, bf16[96,768]{1,0:T(8,128)(2,1)}, bf16[96,768]{1,0:T(8,128)(2,1)}, bf16[96,768]{1,0...) custom-call(s32[2]{0:T(128)S(1)} %pad_add_fusion.members_ref, ...), custom_call_target="tpu_custom_call" | custom-call | flops 50000000 | bytes 100000 | tf_op jit(solution)/shard_map/split/pallas_call | solution.py:54
  176.1 2.6 %collective-permute-start.27 = (bf16[96,768]{1,0:T(8,128)(2,1)}, bf16[96,768]{1,0:T(8,128)(2,1)S(1)}, u32[]{:S(2)}, u32[]{:S(2)}) collective-permute-start(bf16[96,768]{1,0:T(8,128)(2,1)} %get-tuple-element.188), channel_id=1, source_target_pairs={{0,16},{4,20},{8,24},{12,28},{16,0},{20,4},{24,8},{28,12},{1,17},{... | collective-permute-start | bytes 442376 | tf_op jit(solution)/shard_map/ppermute | solution.py:626
  179.3 4.7 %collective-permute-done.32.received_ref = bf16[4,120,768]{2,1,0:T(8,128)(2,1)S(1)} collective-permute-done((bf16[4,120,768]{2,1,0:T(8,128)(2,1)}, bf16[4,120,768]{2,1,0:T(8,128)(2,1)S(1)}, u32[]{:S(2)}, u32[]{:S(2)}) %collective-permute-start.32) | collective-permute-done | bytes 737312 | tf_op jit(solution)/shard_map/ppermute | solution.py:626
  184.9 2.5 %qkv_split.1 = (bf16[120,768]{1,0:T(8,128)(2,1)}, bf16[120,768]{1,0:T(8,128)(2,1)}, bf16[120,768]{1,0:T(8,128)(2,1)}, bf16[120,768]{1,0:T(8,128)(2,1)}) custom-call(s32[2]{0:T(128)S(1)} %pad_add_fusion.members_ref, f32[4,120,768]{2,1,0:T(8,128)} %get-tuple-element.181.kept_ref, bf16[4,120,768]{2,1,0:T(8,128)(2,1)} %copy-done.34), custom_call_target="tpu_custom_call" | custom-call | flops 50000000 | bytes 100000 | tf_op jit(solution)/shard_map/qkv_split/pallas_call | solution.py:54
  192.8 3.1 %collective-permute-start.30 = (bf16[96,768]{1,0:T(8,128)(2,1)S(1)}, bf16[96,768]{1,0:T(8,128)(2,1)S(1)}, u32[]{:S(2)}, u32[]{:S(2)}) collective-permute-start(bf16[96,768]{1,0:T(8,128)(2,1)S(1)} %copy-done.60), channel_id=1, source_target_pairs={{0,16},{4,20},{8,24},{12,28},{16,0},{20,4},{24,8},{28,12},{1,17},{... | collective-permute-start | bytes 442376 | tf_op jit(solution)/shard_map/ppermute | solution.py:626
  197.2 3.7 %sum_in.1 = f32[512,768]{1,0:T(8,128)} custom-call(f32[512,768]{1,0:T(8,128)} %get-tuple-element.151.refs_0_, f32[512,768]{1,0:T(8,128)} %get-tuple-element.156.refs_1_, bf16[512,768]{1,0:T(8,128)(2,1)} %copy-done.31, bf16[512,768]{1,0:T(8,128)(2,1)} %copy-done.32), custom_call_target="tpu_custom_call" | custom-call | flops 50000000 | bytes 100000 | tf_op jit(solution)/shard_map/sum_in/pallas_call | solution.py:54
  200.9 18.0 %collective-permute-done.30.refs_6_ = bf16[96,768]{1,0:T(8,128)(2,1)S(1)} collective-permute-done((bf16[96,768]{1,0:T(8,128)(2,1)S(1)}, bf16[96,768]{1,0:T(8,128)(2,1)S(1)}, u32[]{:S(2)}, u32[]{:S(2)}) %collective-permute-start.30) | collective-permute-done | bytes 147488 | tf_op jit(solution)/shard_map/ppermute | solution.py:626
  218.9 2.5 %collective-permute-done.31.refs_7_ = bf16[96,768]{1,0:T(8,128)(2,1)S(1)} collective-permute-done((bf16[96,768]{1,0:T(8,128)(2,1)S(1)}, bf16[96,768]{1,0:T(8,128)(2,1)S(1)}, u32[]{:S(2)}, u32[]{:S(2)}) %collective-permute-start.31) | collective-permute-done | bytes 147488 | tf_op jit(solution)/shard_map/ppermute | solution.py:626
  222.3 2.6 %finish.1 = (f32[96,192]{1,0:T(8,128)}, f32[96,192]{1,0:T(8,128)}, f32[96,192]{1,0:T(8,128)}, f32[192,96]{1,0:T(8,128)}, f32[1,768]{1,0:T(1,128)S(1)}, /*index=5...) custom-call(bf16[96,768]{1,0:T(8,128)(2,1)} %get-tuple-element.186.refs_0_, bf16[96,768]{1,0:T(8,128)(2,1)} %copy-done.40, ...), custom_call_target="tpu_custom_call" | custom-call | flops 75000000 | bytes 150000 | tf_op jit(solution)/shard_map/finish/pallas_call | solution.py:54
  (201 shorter events, 45.3 us)
Async XLA Ops:
  1.7 11.0 %collective-permute-start = (bf16[192,768]{1,0:T(8,128)(2,1)S(1)}, bf16[192,768]{1,0:T(8,128)(2,1)}, u32[]{:S(2)}, u32[]{:S(2)}) collective-permute-start(bf16[192,768]{1,0:T(8,128)(2,1)S(1)} %constant_dynamic-slice_fusion.1), channel_id=1, source_target_pairs={{0,2},{1,3},{2,0},{3,1},{4,6},{5,7},{6,4},{7,5},{8,10},{9,11},{10,... | collective-permute-start | bytes 884744 | tf_op jit(solution)/shard_map/ppermute | solution.py:621
  6.4 25.9 %collective-permute-start.1 = (bf16[192,768]{1,0:T(8,128)(2,1)}, bf16[192,768]{1,0:T(8,128)(2,1)}, u32[]{:S(2)}, u32[]{:S(2)}) collective-permute-start(bf16[192,768]{1,0:T(8,128)(2,1)} %constant_dynamic-slice_fusion), channel_id=1, source_target_pairs={{0,2},{1,3},{2,0},{3,1},{4,6},{5,7},{6,4},{7,5},{8,10},{9,11},{10,... | collective-permute-start | bytes 884744 | tf_op jit(solution)/shard_map/ppermute | solution.py:621
  12.7 19.8 %collective-permute-start.4 = (bf16[192,768]{1,0:T(8,128)(2,1)}, bf16[192,768]{1,0:T(8,128)(2,1)}, u32[]{:S(2)}, u32[]{:S(2)}) collective-permute-start(bf16[192,768]{1,0:T(8,128)(2,1)} %collective-permute-done.refs_0_), channel_id=1, source_target_pairs={{0,12},{4,8},{8,4},{12,0},{16,28},{20,24},{24,20},{28,16},{1,13},{... | collective-permute-start | bytes 884744 | tf_op jit(solution)/shard_map/ppermute | solution.py:626
  15.7 19.6 %collective-permute-start.3 = (bf16[192,768]{1,0:T(8,128)(2,1)}, bf16[192,768]{1,0:T(8,128)(2,1)}, u32[]{:S(2)}, u32[]{:S(2)}) collective-permute-start(bf16[192,768]{1,0:T(8,128)(2,1)} %collective-permute-done.refs_0_), channel_id=1, source_target_pairs={{0,8},{4,12},{8,0},{12,4},{16,24},{20,28},{24,16},{28,20},{1,9},{5... | collective-permute-start | bytes 884744 | tf_op jit(solution)/shard_map/ppermute | solution.py:626
  16.2 19.6 %collective-permute-start.2 = (bf16[192,768]{1,0:T(8,128)(2,1)}, bf16[192,768]{1,0:T(8,128)(2,1)}, u32[]{:S(2)}, u32[]{:S(2)}) collective-permute-start(bf16[192,768]{1,0:T(8,128)(2,1)} %collective-permute-done.refs_0_), channel_id=1, source_target_pairs={{0,4},{4,0},{8,12},{12,8},{16,20},{20,16},{24,28},{28,24},{1,5},{5... | collective-permute-start | bytes 884744 | tf_op jit(solution)/shard_map/ppermute | solution.py:626
  29.6 18.2 %collective-permute-start.8 = (bf16[1024,192]{1,0:T(8,128)(2,1)}, bf16[1024,192]{1,0:T(8,128)(2,1)}, u32[]{:S(2)}, u32[]{:S(2)}) collective-permute-start(bf16[1024,192]{1,0:T(8,128)(2,1)} %get-tuple-element.113.context_ref), channel_id=1, source_target_pairs={{0,2},{1,3},{2,0},{3,1},{4,6},{5,7},{6,4},{7,5},{8,10},{9,11},{10,... | collective-permute-start | bytes 1179656 | tf_op jit(solution)/shard_map/ppermute | solution.py:621
  32.3 15.5 %collective-permute-start.9 = (bf16[200,768]{1,0:T(8,128)(2,1)}, bf16[200,768]{1,0:T(8,128)(2,1)}, u32[]{:S(2)}, u32[]{:S(2)}) collective-permute-start(bf16[200,768]{1,0:T(8,128)(2,1)} %pad_maximum_fusion), channel_id=1, source_target_pairs={{0,2},{1,3},{2,0},{3,1},{4,6},{5,7},{6,4},{7,5},{8,10},{9,11},{10,... | collective-permute-start | bytes 921608 | tf_op jit(solution)/shard_map/ppermute | solution.py:621
  32.4 13.9 %collective-permute-start.7 = (bf16[192,768]{1,0:T(8,128)(2,1)}, bf16[192,768]{1,0:T(8,128)(2,1)}, u32[]{:S(2)}, u32[]{:S(2)}) collective-permute-start(bf16[192,768]{1,0:T(8,128)(2,1)} %collective-permute-done.1.refs_0_), channel_id=1, source_target_pairs={{0,12},{4,8},{8,4},{12,0},{16,28},{20,24},{24,20},{28,16},{1,13},{... | collective-permute-start | bytes 884744 | tf_op jit(solution)/shard_map/ppermute | solution.py:626
  35.3 11.0 %collective-permute-start.6 = (bf16[192,768]{1,0:T(8,128)(2,1)}, bf16[192,768]{1,0:T(8,128)(2,1)}, u32[]{:S(2)}, u32[]{:S(2)}) collective-permute-start(bf16[192,768]{1,0:T(8,128)(2,1)} %collective-permute-done.1.refs_0_), channel_id=1, source_target_pairs={{0,8},{4,12},{8,0},{12,4},{16,24},{20,28},{24,16},{28,20},{1,9},{5... | collective-permute-start | bytes 884744 | tf_op jit(solution)/shard_map/ppermute | solution.py:626
  35.8 10.6 %collective-permute-start.5 = (bf16[192,768]{1,0:T(8,128)(2,1)}, bf16[192,768]{1,0:T(8,128)(2,1)}, u32[]{:S(2)}, u32[]{:S(2)}) collective-permute-start(bf16[192,768]{1,0:T(8,128)(2,1)} %collective-permute-done.1.refs_0_), channel_id=1, source_target_pairs={{0,4},{4,0},{8,12},{12,8},{16,20},{20,16},{24,28},{28,24},{1,5},{5... | collective-permute-start | bytes 884744 | tf_op jit(solution)/shard_map/ppermute | solution.py:626
  49.9 2.4 %collective-permute-start.10 = (bf16[512,768]{1,0:T(8,128)(2,1)S(1)}, bf16[512,768]{1,0:T(8,128)(2,1)S(1)}, u32[]{:S(2)}, u32[]{:S(2)}) collective-permute-start(bf16[512,768]{1,0:T(8,128)(2,1)S(1)} %get-tuple-element.118), channel_id=1, source_target_pairs={{0,1},{1,0},{2,3},{3,2},{4,5},{5,4},{6,7},{7,6},{8,9},{9,8},{10,11... | collective-permute-start | bytes 2359304 | tf_op jit(solution)/shard_map/ppermute | solution.py:621
  70.1 2.4 %collective-permute-start.12 = (bf16[512,768]{1,0:T(8,128)(2,1)S(1)}, bf16[512,768]{1,0:T(8,128)(2,1)S(1)}, u32[]{:S(2)}, u32[]{:S(2)}) collective-permute-start(bf16[512,768]{1,0:T(8,128)(2,1)S(1)} %get-tuple-element.125), channel_id=1, source_target_pairs={{0,1},{1,0},{2,3},{3,2},{4,5},{5,4},{6,7},{7,6},{8,9},{9,8},{10,11... | collective-permute-start | bytes 2359304 | tf_op jit(solution)/shard_map/ppermute | solution.py:621
  86.9 15.9 %collective-permute-start.14 = (bf16[512,768]{1,0:T(8,128)(2,1)}, bf16[512,768]{1,0:T(8,128)(2,1)}, u32[]{:S(2)}, u32[]{:S(2)}) collective-permute-start(bf16[512,768]{1,0:T(8,128)(2,1)} %get-tuple-element.146), channel_id=1, source_target_pairs={{0,1},{1,0},{2,3},{3,2},{4,5},{5,4},{6,7},{7,6},{8,9},{9,8},{10,11... | collective-permute-start | bytes 2359304 | tf_op jit(solution)/shard_map/ppermute | solution.py:621
  106.7 4.9 %collective-permute-start.15 = (bf16[536,768]{1,0:T(8,128)(2,1)}, bf16[536,768]{1,0:T(8,128)(2,1)S(1)}, u32[]{:S(2)}, u32[]{:S(2)}) collective-permute-start(bf16[536,768]{1,0:T(8,128)(2,1)} %get-tuple-element.152.first_ref.mine_ref), channel_id=1, source_target_pairs={{0,1},{1,0},{2,3},{3,2},{4,5},{5,4},{6,7},{7,6},{8,9},{9,8},{10,11... | collective-permute-start | bytes 2469896 | tf_op jit(solution)/shard_map/ppermute | solution.py:621
  107.1 19.2 %collective-permute-start.16 = (bf16[4,96,768]{2,1,0:T(8,128)(2,1)S(1)}, bf16[4,96,768]{2,1,0:T(8,128)(2,1)S(1)}, u32[]{:S(2)}, u32[]{:S(2)}) collective-permute-start(bf16[4,96,768]{2,1,0:T(8,128)(2,1)S(1)} %copy-done.55), channel_id=1, source_target_pairs={{0,4},{4,0},{8,12},{12,8},{16,20},{20,16},{24,28},{28,24},{1,5},{5... | collective-permute-start | bytes 1769480 | tf_op jit(solution)/shard_map/ppermute | solution.py:626
  108.6 17.8 %collective-permute-start.17 = (bf16[4,96,768]{2,1,0:T(8,128)(2,1)S(1)}, bf16[4,96,768]{2,1,0:T(8,128)(2,1)S(1)}, u32[]{:S(2)}, u32[]{:S(2)}) collective-permute-start(bf16[4,96,768]{2,1,0:T(8,128)(2,1)S(1)} %copy-done.56), channel_id=1, source_target_pairs={{0,8},{4,12},{8,0},{12,4},{16,24},{20,28},{24,16},{28,20},{1,9},{5... | collective-permute-start | bytes 1769480 | tf_op jit(solution)/shard_map/ppermute | solution.py:626
  110.1 21.1 %collective-permute-start.19 = (bf16[536,768]{1,0:T(8,128)(2,1)}, bf16[536,768]{1,0:T(8,128)(2,1)S(1)}, u32[]{:S(2)}, u32[]{:S(2)}) collective-permute-start(bf16[536,768]{1,0:T(8,128)(2,1)} %get-tuple-element.152.first_ref.mine_ref), channel_id=1, source_target_pairs={{0,2},{1,3},{2,0},{3,1},{4,6},{5,7},{6,4},{7,5},{8,10},{9,11},{10,... | collective-permute-start | bytes 2469896 | tf_op jit(solution)/shard_map/ppermute | solution.py:621
  130.7 27.4 %collective-permute-start.23 = (bf16[8,96,768]{2,1,0:T(8,128)(2,1)}, bf16[8,96,768]{2,1,0:T(8,128)(2,1)S(1)}, u32[]{:S(2)}, u32[]{:S(2)}) collective-permute-start(bf16[8,96,768]{2,1,0:T(8,128)(2,1)} %combine.1), channel_id=1, source_target_pairs={{0,2},{1,3},{2,0},{3,1},{4,6},{5,7},{6,4},{7,5},{8,10},{9,11},{10,... | collective-permute-start | bytes 3538952 | tf_op jit(solution)/shard_map/ppermute | solution.py:621
  131.3 16.6 %collective-permute-start.21 = (bf16[4,96,768]{2,1,0:T(8,128)(2,1)S(1)}, bf16[4,96,768]{2,1,0:T(8,128)(2,1)S(1)}, u32[]{:S(2)}, u32[]{:S(2)}) collective-permute-start(bf16[4,96,768]{2,1,0:T(8,128)(2,1)S(1)} %copy-done.53), channel_id=1, source_target_pairs={{0,4},{4,0},{8,12},{12,8},{16,20},{20,16},{24,28},{28,24},{1,5},{5... | collective-permute-start | bytes 1769480 | tf_op jit(solution)/shard_map/ppermute | solution.py:626
  131.9 16.0 %collective-permute-start.22 = (bf16[4,96,768]{2,1,0:T(8,128)(2,1)S(1)}, bf16[4,96,768]{2,1,0:T(8,128)(2,1)S(1)}, u32[]{:S(2)}, u32[]{:S(2)}) collective-permute-start(bf16[4,96,768]{2,1,0:T(8,128)(2,1)S(1)} %copy-done.54), channel_id=1, source_target_pairs={{0,8},{4,12},{8,0},{12,4},{16,24},{20,28},{24,16},{28,20},{1,9},{5... | collective-permute-start | bytes 1769480 | tf_op jit(solution)/shard_map/ppermute | solution.py:626
  164.8 13.9 %collective-permute-start.18 = (bf16[512,768]{1,0:T(8,128)(2,1)}, bf16[512,768]{1,0:T(8,128)(2,1)S(1)}, u32[]{:S(2)}, u32[]{:S(2)}) collective-permute-start(bf16[512,768]{1,0:T(8,128)(2,1)} %get-tuple-element.162), channel_id=1, source_target_pairs={{0,1},{1,0},{2,3},{3,2},{4,5},{5,4},{6,7},{7,6},{8,9},{9,8},{10,11... | collective-permute-start | bytes 2359304 | tf_op jit(solution)/shard_map/ppermute | solution.py:621
  165.3 18.7 %collective-permute-start.32 = (bf16[4,120,768]{2,1,0:T(8,128)(2,1)}, bf16[4,120,768]{2,1,0:T(8,128)(2,1)S(1)}, u32[]{:S(2)}, u32[]{:S(2)}) collective-permute-start(bf16[4,120,768]{2,1,0:T(8,128)(2,1)} %get-tuple-element.194), channel_id=1, source_target_pairs={{0,4},{4,0},{8,12},{12,8},{16,20},{20,16},{24,28},{28,24},{1,5},{5... | collective-permute-start | bytes 2211848 | tf_op jit(solution)/shard_map/ppermute | solution.py:626
  170.6 25.3 %collective-permute-start.25 = (bf16[512,768]{1,0:T(8,128)(2,1)}, bf16[512,768]{1,0:T(8,128)(2,1)S(1)}, u32[]{:S(2)}, u32[]{:S(2)}) collective-permute-start(bf16[512,768]{1,0:T(8,128)(2,1)} %sum_far.1), channel_id=1, source_target_pairs={{0,2},{1,3},{2,0},{3,1},{4,6},{5,7},{6,4},{7,5},{8,10},{9,11},{10,... | collective-permute-start | bytes 2359304 | tf_op jit(solution)/shard_map/ppermute | solution.py:621
  174.9 12.5 %collective-permute-start.26 = (bf16[96,768]{1,0:T(8,128)(2,1)}, bf16[96,768]{1,0:T(8,128)(2,1)S(1)}, u32[]{:S(2)}, u32[]{:S(2)}) collective-permute-start(bf16[96,768]{1,0:T(8,128)(2,1)} %get-tuple-element.187), channel_id=1, source_target_pairs={{0,8},{4,12},{8,0},{12,4},{16,24},{20,28},{24,16},{28,20},{1,9},{5... | collective-permute-start | bytes 442376 | tf_op jit(solution)/shard_map/ppermute | solution.py:626
  176.1 14.1 %collective-permute-start.27 = (bf16[96,768]{1,0:T(8,128)(2,1)}, bf16[96,768]{1,0:T(8,128)(2,1)S(1)}, u32[]{:S(2)}, u32[]{:S(2)}) collective-permute-start(bf16[96,768]{1,0:T(8,128)(2,1)} %get-tuple-element.188), channel_id=1, source_target_pairs={{0,16},{4,20},{8,24},{12,28},{16,0},{20,4},{24,8},{28,12},{1,17},{... | collective-permute-start | bytes 442376 | tf_op jit(solution)/shard_map/ppermute | solution.py:626
  178.7 12.2 %collective-permute-start.28 = (bf16[96,768]{1,0:T(8,128)(2,1)}, bf16[96,768]{1,0:T(8,128)(2,1)S(1)}, u32[]{:S(2)}, u32[]{:S(2)}) collective-permute-start(bf16[96,768]{1,0:T(8,128)(2,1)} %get-tuple-element.189), channel_id=1, source_target_pairs={{0,24},{4,28},{8,16},{12,20},{16,8},{20,12},{24,0},{28,4},{1,25},{... | collective-permute-start | bytes 442376 | tf_op jit(solution)/shard_map/ppermute | solution.py:626
  184.0 8.8 %collective-permute-start.29 = (bf16[96,768]{1,0:T(8,128)(2,1)}, bf16[96,768]{1,0:T(8,128)(2,1)S(1)}, u32[]{:S(2)}, u32[]{:S(2)}) collective-permute-start(bf16[96,768]{1,0:T(8,128)(2,1)} %get-tuple-element.191), channel_id=1, source_target_pairs={{0,4},{4,0},{8,12},{12,8},{16,20},{20,16},{24,28},{28,24},{1,5},{5... | collective-permute-start | bytes 442376 | tf_op jit(solution)/shard_map/ppermute | solution.py:626
  187.4 34.1 %collective-permute-start.33 = (bf16[120,768]{1,0:T(8,128)(2,1)}, bf16[120,768]{1,0:T(8,128)(2,1)S(1)}, u32[]{:S(2)}, u32[]{:S(2)}) collective-permute-start(bf16[120,768]{1,0:T(8,128)(2,1)} %get-tuple-element.196), channel_id=1, source_target_pairs={{0,8},{4,12},{8,0},{12,4},{16,24},{20,28},{24,16},{28,20},{1,9},{5... | collective-permute-start | bytes 552968 | tf_op jit(solution)/shard_map/ppermute | solution.py:626
  190.3 31.2 %collective-permute-start.34 = (bf16[120,768]{1,0:T(8,128)(2,1)}, bf16[120,768]{1,0:T(8,128)(2,1)S(1)}, u32[]{:S(2)}, u32[]{:S(2)}) collective-permute-start(bf16[120,768]{1,0:T(8,128)(2,1)} %get-tuple-element.197), channel_id=1, source_target_pairs={{0,16},{4,20},{8,24},{12,28},{16,0},{20,4},{24,8},{28,12},{1,17},{... | collective-permute-start | bytes 552968 | tf_op jit(solution)/shard_map/ppermute | solution.py:626
  190.9 30.6 %collective-permute-start.35 = (bf16[120,768]{1,0:T(8,128)(2,1)}, bf16[120,768]{1,0:T(8,128)(2,1)S(1)}, u32[]{:S(2)}, u32[]{:S(2)}) collective-permute-start(bf16[120,768]{1,0:T(8,128)(2,1)} %get-tuple-element.198), channel_id=1, source_target_pairs={{0,24},{4,28},{8,16},{12,20},{16,8},{20,12},{24,0},{28,4},{1,25},{... | collective-permute-start | bytes 552968 | tf_op jit(solution)/shard_map/ppermute | solution.py:626
  192.8 26.1 %collective-permute-start.30 = (bf16[96,768]{1,0:T(8,128)(2,1)S(1)}, bf16[96,768]{1,0:T(8,128)(2,1)S(1)}, u32[]{:S(2)}, u32[]{:S(2)}) collective-permute-start(bf16[96,768]{1,0:T(8,128)(2,1)S(1)} %copy-done.60), channel_id=1, source_target_pairs={{0,16},{4,20},{8,24},{12,28},{16,0},{20,4},{24,8},{28,12},{1,17},{... | collective-permute-start | bytes 442376 | tf_op jit(solution)/shard_map/ppermute | solution.py:626
  195.9 25.5 %collective-permute-start.31 = (bf16[96,768]{1,0:T(8,128)(2,1)S(1)}, bf16[96,768]{1,0:T(8,128)(2,1)S(1)}, u32[]{:S(2)}, u32[]{:S(2)}) collective-permute-start(bf16[96,768]{1,0:T(8,128)(2,1)S(1)} %copy-done.59), channel_id=1, source_target_pairs={{0,20},{4,16},{8,28},{12,24},{16,4},{20,0},{24,12},{28,8},{1,21},{... | collective-permute-start | bytes 442376 | tf_op jit(solution)/shard_map/ppermute | solution.py:626
  (65 other events, 536.9 us)
